TPU v7x, 256 devices: a 4x2x16 block of a 4x16x16 slice. The times are simulated.
256 devices in a mesh: groups: 2 (over y), blk: 128 (over z, x, core).
Axes of the slice: x: 4, y: 2, z: 16, core: 2. Of those that a mesh axis runs over, the one named last changes fastest.
The devices are a block of a 4x16x16 slice.
Arguments:
- positions: float32 [3, 65536], P(None, ('groups', 'blk')), parts along dimension 1, may hold values from 0 to 96
- right_side: float32 [3, 65536], P(None, ('groups', 'blk')), parts along dimension 1, may hold values from -18 to 18
- neighbours: int32 [16, 65536], P(None, ('groups', 'blk')), parts along dimension 1, may hold values from 0 to 32767, as said below
- counts: int32 [65536], P(('groups', 'blk')), parts along dimension 0, may hold values from 1 to 16
Outputs:
- solution: float32 [3, 65536], P(None, ('groups', 'blk')), parts along dimension 1
- residual: float32 [3, 65536], P(None, ('groups', 'blk')), parts along dimension 1
There are 2 independent parts, one for each index of `groups`. A program takes and returns all parts, laid end to end along the dimension named above; each array names one. Nothing has to cross between parts.
Inputs may be any that keep to these rules, and one draw needn't show every extreme that they name: `neighbours`: every entry in column i lies within 32 of i, counted cyclically over the 32768 particles.
All inputs are finite; a program needn't handle non-finite values.
Results may differ from a plain program's by a relative error of at most 0.0003.
Values sent between devices are 32-bit elements; how exact they have to be, the bound alone decides.
A program may use at most 64 MiB of HBM per device.

v0:
```python
import functools
import math

import jax
import jax.numpy as jnp
from jax import lax
from jax.sharding import Mesh
from jax.sharding import PartitionSpec as P

REACH = 32
ITERS = 2
BLK = ("blk_0", "blk_1", "blk_2")
GROUPS_BLK = ("groups", "blk_0", "blk_1", "blk_2")


SOFT = 0.0001
EPS = 1e-06


def extended_2(cells, sides, width):
    for axis, dim in sides:
        count = lax.axis_size(axis)
        head = lax.slice_in_dim(cells, 0, width, axis=dim)
        tail = lax.slice_in_dim(cells, cells.shape[dim] - width, cells.shape[dim], axis=dim)
        cells = jnp.concatenate(
            [
                lax.ppermute(tail, axis, [(i, (i + 1) % count) for i in range(count)]),
                cells,
                lax.ppermute(head, axis, [((i + 1) % count, i) for i in range(count)]),
            ],
            axis=dim,
        )
    return cells


def joined_along(tiles, dim):
    lengths = list(tiles.shape[1:])
    lengths[dim] *= tiles.shape[0]
    return jnp.moveaxis(tiles, 0, dim).reshape(lengths)


def stacked_from(array, axes, turns):
    tiles = array[None]
    for k in turns:
        tiles = lax.all_gather(tiles, axes[k], axis=0, tiled=True)
    held = [lax.axis_size(axes[k]) for k in reversed(turns)]
    tiles = tiles.reshape(*held, *array.shape)
    turned = sorted(range(len(turns)), key=lambda place: turns[len(turns) - 1 - place])
    return tiles.transpose(*turned, *range(len(turns), tiles.ndim)).reshape(-1, *array.shape)


def gathered_by_axis(array, axes, turns, dim):
    return joined_along(stacked_from(array, axes, turns), dim)


def one_axis_at_a_time(array, axes):
    return functools.reduce(lax.psum, axes, array)


def pair_coefficients(dx, dy, dz):
    dist = jnp.sqrt(dx * dx + dy * dy + dz * dz + SOFT)
    inverse = 1.0 / dist
    cube = inverse * inverse * inverse
    correlation = dist < 2.0
    coef_a = jnp.where(correlation, 1.0 - 9.0 * dist / 32.0, 0.75 * inverse + 0.5 * cube)
    coef_b = jnp.where(
        correlation, 3.0 / 32.0 * inverse, 0.75 * cube - 1.5 * cube * inverse * inverse
    )
    return (coef_a, coef_b)


def far_tile(row_pos, col_pos, col_vec):
    dx = row_pos[0][:, None] - col_pos[0][None, :]
    dy = row_pos[1][:, None] - col_pos[1][None, :]
    dz = row_pos[2][:, None] - col_pos[2][None, :]
    coef_a, coef_b = pair_coefficients(dx, dy, dz)
    along = dx * col_vec[0][None, :] + dy * col_vec[1][None, :] + dz * col_vec[2][None, :]
    weighted = coef_b * along
    out_x = jnp.sum(coef_a * col_vec[0][None, :] + weighted * dx, axis=1)
    out_y = jnp.sum(coef_a * col_vec[1][None, :] + weighted * dy, axis=1)
    out_z = jnp.sum(coef_a * col_vec[2][None, :] + weighted * dz, axis=1)
    return jnp.stack([out_x, out_y, out_z])


def far_piece(row_pos, col_pos, col_vec):
    width = col_pos.shape[1]
    size = math.gcd(width, 4096)
    count = width // size
    stacked_pos = col_pos.reshape(3, count, size).transpose(1, 0, 2)
    stacked_vec = col_vec.reshape(3, count, size).transpose(1, 0, 2)

    def advance(carry, item):
        return (carry + far_tile(row_pos, item[0], item[1]), None)

    start_sum = jnp.zeros((3, row_pos.shape[1]), jnp.float32)
    result, unused = lax.scan(advance, start_sum, (stacked_pos, stacked_vec))
    return result


def lubrication(positions, vec, near_pos, near_vec, live):
    delta = positions[:, None, :] - near_pos
    square = jnp.sum(delta * delta, axis=0) + SOFT
    dist = jnp.sqrt(square)
    strength = live / ((0.5 + jnp.abs(dist - 2.0)) * square)
    along = jnp.sum(delta * (vec[:, None, :] - near_vec), axis=0)
    return jnp.sum(delta * (strength * along)[None], axis=1)


def on_device(positions, right_side, neighbours, counts):
    rows = positions.shape[1]
    blocks = lax.axis_size(BLK)
    total = rows * blocks
    first_row = lax.axis_index(BLK) * rows
    slots = jnp.arange(neighbours.shape[0], dtype=jnp.int32)
    live = (slots[:, None] < counts[None, :]).astype(jnp.float32)
    local_slot = jnp.remainder(neighbours - first_row + REACH, total)
    beta = jnp.sqrt(one_axis_at_a_time(jnp.sum(right_side * right_side), BLK) + EPS)
    basis = [right_side / beta]
    images = []
    cosines = []
    sines = []
    rotated = [beta]
    columns = []
    for step in range(ITERS):
        vec = basis[step]
        stacked = jnp.concatenate([positions, vec], axis=0)
        extended = extended_2(stacked, ((BLK, 1),), REACH)
        picked = jnp.take(extended, local_slot, axis=1)
        gathered = gathered_by_axis(stacked, BLK, (1, 0, 2), 1)
        far = far_piece(positions, gathered[:3], gathered[3:])
        work = far + lubrication(positions, vec, picked[:3], picked[3:], live)
        images.append(work)
        local_terms = tuple((jnp.sum(work * basis[j]) for j in range(step + 1))) + (
            jnp.sum(work * work),
        )
        totals = jax.tree.map(lambda part: one_axis_at_a_time(part, BLK), local_terms)
        column = list(totals[: step + 1])
        squares = totals[step + 1]
        for j in range(step + 1):
            work = work - column[j] * basis[j]
            squares = squares - column[j] * column[j]
        below = jnp.sqrt(squares + EPS)
        basis.append(work / below)
        column.append(below)
        for j in range(step):
            first, second = (column[j], column[j + 1])
            column[j] = cosines[j] * first + sines[j] * second
            column[j + 1] = -sines[j] * first + cosines[j] * second
        pivot = jnp.sqrt(column[step] * column[step] + below * below)
        cosines.append(column[step] / pivot)
        sines.append(below / pivot)
        column[step] = pivot
        rotated.append(-sines[step] * rotated[step])
        rotated[step] = cosines[step] * rotated[step]
        columns.append(column)
    coeffs = [None] * ITERS
    for step in reversed(range(ITERS)):
        accum = rotated[step]
        for j in range(step + 1, ITERS):
            accum = accum - columns[j][step] * coeffs[j]
        coeffs[step] = accum / columns[step][step]
    solution = jnp.zeros_like(right_side)
    residual = right_side
    for step in range(ITERS):
        solution = solution + coeffs[step] * basis[step]
        residual = residual - coeffs[step] * images[step]
    return (solution, residual)


def solution(mesh):
    torus = Mesh(
        mesh.devices.reshape(mesh.shape["groups"], 16, 4, 2), ("groups", "blk_0", "blk_1", "blk_2")
    )
    placed = (P(None, GROUPS_BLK), P(None, GROUPS_BLK), P(None, GROUPS_BLK), P(GROUPS_BLK))
    return jax.shard_map(
        on_device,
        mesh=torus,
        in_specs=placed,
        out_specs=(P(None, GROUPS_BLK), P(None, GROUPS_BLK)),
        check_vma=False,
    )
```

profile of v0, /device:TPU:40, one launch (start us, length us, event | category | flops | bytes accessed | tf_op | source)
XLA Modules:
  0.0 428.3 jit_solution(15191888906879357911)
XLA Ops:
  0.6 1.3 multiply_reduce_fusion.9
  1.9 50.0 %psum.126 = f32[]{:T(128)} all-reduce(f32[]{:T(128)} %multiply_reduce_fusion.9), channel_id=1, replica_groups=mesh['groups'=2,'blk_0'=16,'blk_1'=4,'blk_2'=2] {'blk_0'}, use_global_device_ids=true, to_apply=%region_1.2 | all-reduce | flops 1 | bytes 8 | tf_op jit(solution)/shard_map/psum | solution.py:57
  52.0 11.5 %psum.127 = f32[]{:T(128)} all-reduce(f32[]{:T(128)} %psum.126), channel_id=1, replica_groups=mesh['groups'=2,'blk_0'=16,'blk_1'=4,'blk_2'=2] {'blk_1'}, use_global_device_ids=true, to_apply=%region_2.3 | all-reduce | flops 1 | bytes 8 | tf_op jit(solution)/shard_map/psum | solution.py:57
  63.5 3.1 psum.128
  67.3 0.7 broadcast_divide_fusion
  68.0 0.8 fusion.55
  68.7 0.2 collective-permute-start
  69.0 4.9 %collective-permute-start.1 = (f32[6,32]{1,0:T(8,128)S(1)}, f32[6,32]{1,0:T(8,128)S(1)}, u32[]{:S(2)}, u32[]{:S(2)}) collective-permute-start(f32[6,32]{1,0:T(8,128)S(1)} %get-tuple-element.262), channel_id=1, source_target_pairs={{1,0},{2,1},{3,2},{4,3},{5,4},{6,5},{7,6},{8,7},{9,8},{10,9},{11,1... | collective-permute-start | bytes 2312 | tf_op jit(solution)/shard_map/ppermute | solution.py:29
  73.9 0.7 fusion.51
  74.6 0.7 fusion.57
  75.3 12.0 %all-gather.2 = f32[4,6,256]{2,1,0:T(8,128)S(1)} all-gather(f32[1,6,256]{2,1,0:T(8,128)S(1)} %fusion.51), channel_id=2, replica_groups=mesh['groups'=2,'blk_0'=16,'blk_1'=4,'blk_2'=2] {'blk_1'}, dimensions={0}, use_global_device_ids=true | all-gather | bytes 30720 | tf_op jit(solution)/shard_map/all_gather | solution.py:45
  87.3 28.8 %all_gather.19 = f32[64,6,256]{2,1,0:T(8,128)S(1)} all-gather(f32[4,6,256]{2,1,0:T(8,128)S(1)} %all-gather.2), channel_id=1, replica_groups=mesh['groups'=2,'blk_0'=16,'blk_1'=4,'blk_2'=2] {'blk_0'}, dimensions={0}, use_global_device_ids=true | all-gather | bytes 417792 | tf_op jit(solution)/shard_map/all_gather | solution.py:45
  116.2 2.6 all_gather.20
  118.8 0.2 reshape.139
  119.0 0.6 copy.108
  119.7 0.5 reshape.140
  120.5 0.5 copy_bitcast_fusion.4
  121.0 66.1 %while.26 = (s32[]{:T(128)}, f32[3,256]{1,0:T(4,128)S(1)}, f32[3,256]{1,0:T(4,128)S(1)}, f32[8,3,4096]{2,1,0:T(4,128)S(1)}, f32[8,3,4096]{2,1,0:T(4,128)S(1)}, /*index=5*/s32[]{:T(128)}, s32[]{:T(128)}, s32[]{}, s32[]{}) while((s32[]{:T(128)}, f32[3,256]{1,0:T(4,128)S(1)}, f32[3,256]{1,0:T(4,128)S(1)}, ...), condition=%wide.region_8.9_spmd.clone, body=%wide.region_4.0_spmd.clone.sunk | while | flops 46139652 | bytes 316555 | solution.py:96
  121.2 8.1 %fusion.67 = (f32[256]{0:T(256)S(1)}, f32[256]{0:T(256)S(1)}, f32[256]{0:T(256)S(1)}) fusion(f32[4096]{0:T(1024)S(1)} %bitcast.120, f32[4096]{0:T(1024)S(1)} %bitcast.123, f32[256]{0:T(256)S(1)} %bitcast.140, f32[4096]{0:T(1024)S(1)} %bitcast.122, f32[256]{0:T(256)S(1)} %bitcast.139, f32[4096]{0:T(1024)S(1)} %bitcast.124, f32[256]{0:T(256)S(1)} %bitcast.138, ...), kind=kLoop, calls=%fused_computation.23.clone.1 | loop fusion | flops 46136576 | bytes 104448 | tf_op jit(solution)/shard_map/while/body/eval_jaxpr/reduce_sum | solution.py:79
  129.4 8.1 %fusion.67 = (f32[256]{0:T(256)S(1)}, f32[256]{0:T(256)S(1)}, f32[256]{0:T(256)S(1)}) fusion(f32[4096]{0:T(1024)S(1)} %bitcast.120, f32[4096]{0:T(1024)S(1)} %bitcast.123, f32[256]{0:T(256)S(1)} %bitcast.140, f32[4096]{0:T(1024)S(1)} %bitcast.122, f32[256]{0:T(256)S(1)} %bitcast.139, f32[4096]{0:T(1024)S(1)} %bitcast.124, f32[256]{0:T(256)S(1)} %bitcast.138, ...), kind=kLoop, calls=%fused_computation.23.clone.1 | loop fusion | flops 46136576 | bytes 104448 | tf_op jit(solution)/shard_map/while/body/eval_jaxpr/reduce_sum | solution.py:79
  137.7 8.1 %fusion.67 = (f32[256]{0:T(256)S(1)}, f32[256]{0:T(256)S(1)}, f32[256]{0:T(256)S(1)}) fusion(f32[4096]{0:T(1024)S(1)} %bitcast.120, f32[4096]{0:T(1024)S(1)} %bitcast.123, f32[256]{0:T(256)S(1)} %bitcast.140, f32[4096]{0:T(1024)S(1)} %bitcast.122, f32[256]{0:T(256)S(1)} %bitcast.139, f32[4096]{0:T(1024)S(1)} %bitcast.124, f32[256]{0:T(256)S(1)} %bitcast.138, ...), kind=kLoop, calls=%fused_computation.23.clone.1 | loop fusion | flops 46136576 | bytes 104448 | tf_op jit(solution)/shard_map/while/body/eval_jaxpr/reduce_sum | solution.py:79
  146.0 8.1 %fusion.67 = (f32[256]{0:T(256)S(1)}, f32[256]{0:T(256)S(1)}, f32[256]{0:T(256)S(1)}) fusion(f32[4096]{0:T(1024)S(1)} %bitcast.120, f32[4096]{0:T(1024)S(1)} %bitcast.123, f32[256]{0:T(256)S(1)} %bitcast.140, f32[4096]{0:T(1024)S(1)} %bitcast.122, f32[256]{0:T(256)S(1)} %bitcast.139, f32[4096]{0:T(1024)S(1)} %bitcast.124, f32[256]{0:T(256)S(1)} %bitcast.138, ...), kind=kLoop, calls=%fused_computation.23.clone.1 | loop fusion | flops 46136576 | bytes 104448 | tf_op jit(solution)/shard_map/while/body/eval_jaxpr/reduce_sum | solution.py:79
  154.2 8.1 %fusion.67 = (f32[256]{0:T(256)S(1)}, f32[256]{0:T(256)S(1)}, f32[256]{0:T(256)S(1)}) fusion(f32[4096]{0:T(1024)S(1)} %bitcast.120, f32[4096]{0:T(1024)S(1)} %bitcast.123, f32[256]{0:T(256)S(1)} %bitcast.140, f32[4096]{0:T(1024)S(1)} %bitcast.122, f32[256]{0:T(256)S(1)} %bitcast.139, f32[4096]{0:T(1024)S(1)} %bitcast.124, f32[256]{0:T(256)S(1)} %bitcast.138, ...), kind=kLoop, calls=%fused_computation.23.clone.1 | loop fusion | flops 46136576 | bytes 104448 | tf_op jit(solution)/shard_map/while/body/eval_jaxpr/reduce_sum | solution.py:79
  162.5 8.1 %fusion.67 = (f32[256]{0:T(256)S(1)}, f32[256]{0:T(256)S(1)}, f32[256]{0:T(256)S(1)}) fusion(f32[4096]{0:T(1024)S(1)} %bitcast.120, f32[4096]{0:T(1024)S(1)} %bitcast.123, f32[256]{0:T(256)S(1)} %bitcast.140, f32[4096]{0:T(1024)S(1)} %bitcast.122, f32[256]{0:T(256)S(1)} %bitcast.139, f32[4096]{0:T(1024)S(1)} %bitcast.124, f32[256]{0:T(256)S(1)} %bitcast.138, ...), kind=kLoop, calls=%fused_computation.23.clone.1 | loop fusion | flops 46136576 | bytes 104448 | tf_op jit(solution)/shard_map/while/body/eval_jaxpr/reduce_sum | solution.py:79
  170.7 8.1 %fusion.67 = (f32[256]{0:T(256)S(1)}, f32[256]{0:T(256)S(1)}, f32[256]{0:T(256)S(1)}) fusion(f32[4096]{0:T(1024)S(1)} %bitcast.120, f32[4096]{0:T(1024)S(1)} %bitcast.123, f32[256]{0:T(256)S(1)} %bitcast.140, f32[4096]{0:T(1024)S(1)} %bitcast.122, f32[256]{0:T(256)S(1)} %bitcast.139, f32[4096]{0:T(1024)S(1)} %bitcast.124, f32[256]{0:T(256)S(1)} %bitcast.138, ...), kind=kLoop, calls=%fused_computation.23.clone.1 | loop fusion | flops 46136576 | bytes 104448 | tf_op jit(solution)/shard_map/while/body/eval_jaxpr/reduce_sum | solution.py:79
  179.0 8.1 %fusion.67 = (f32[256]{0:T(256)S(1)}, f32[256]{0:T(256)S(1)}, f32[256]{0:T(256)S(1)}) fusion(f32[4096]{0:T(1024)S(1)} %bitcast.120, f32[4096]{0:T(1024)S(1)} %bitcast.123, f32[256]{0:T(256)S(1)} %bitcast.140, f32[4096]{0:T(1024)S(1)} %bitcast.122, f32[256]{0:T(256)S(1)} %bitcast.139, f32[4096]{0:T(1024)S(1)} %bitcast.124, f32[256]{0:T(256)S(1)} %bitcast.138, ...), kind=kLoop, calls=%fused_computation.23.clone.1 | loop fusion | flops 46136576 | bytes 104448 | tf_op jit(solution)/shard_map/while/body/eval_jaxpr/reduce_sum | solution.py:79
  187.7 10.8 %gather_fusion = f32[4096,6]{1,0:T(8,128)S(1)} fusion(f32[6,320]{0,1:T(8,128)S(1)} %copy.90, s32[4096]{0:T(1024)S(1)} %broadcast_clamp_fusion), kind=kCustom, calls=%fused_computation.clone | custom fusion | bytes 212992 | tf_op jit(solution)/shard_map/jit(_take)/gather | solution.py:128
  198.5 0.7 select_bitcast_fusion.1
  199.2 1.7 multiply_reduce_fusion.3
  201.0 0.7 multiply_reduce_fusion.2
  201.8 0.6 multiply_reduce_fusion.8
  202.5 29.6 %all-reduce.1 = (f32[]{:T(128)}, f32[]{:T(128)}) all-reduce(f32[]{:T(128)} %get-tuple-element.193, f32[]{:T(128)} %get-tuple-element.192), channel_id=1, replica_groups=mesh['groups'=2,'blk_0'=16,'blk_1'=4,'blk_2'=2] {'blk_0'}, use_global_device_ids=true, to_apply=%region_17.19 | all-reduce | flops 2 | bytes 16 | tf_op jit(solution)/shard_map/psum | solution.py:57
  232.1 8.6 %all-reduce.3 = (f32[]{:T(128)}, f32[]{:T(128)}) all-reduce(f32[]{:T(128)} %get-tuple-element.217, f32[]{:T(128)} %get-tuple-element.218), channel_id=1, replica_groups=mesh['groups'=2,'blk_0'=16,'blk_1'=4,'blk_2'=2] {'blk_1'}, use_global_device_ids=true, to_apply=%region_18.20 | all-reduce | flops 2 | bytes 16 | tf_op jit(solution)/shard_map/psum | solution.py:57
  240.7 3.1 all-reduce.5
  245.8 0.7 subtract_divide_fusion
  246.5 0.3 collective-permute-start.2
  246.8 4.9 %collective-permute-start.3 = (f32[6,32]{1,0:T(8,128)S(1)}, f32[6,32]{1,0:T(8,128)S(1)}, u32[]{:S(2)}, u32[]{:S(2)}) collective-permute-start(f32[6,32]{1,0:T(8,128)S(1)} %get-tuple-element.260), channel_id=1, source_target_pairs={{1,0},{2,1},{3,2},{4,3},{5,4},{6,5},{7,6},{8,7},{9,8},{10,9},{11,1... | collective-permute-start | bytes 2312 | tf_op jit(solution)/shard_map/ppermute | solution.py:29
  251.7 12.2 %all-gather.3 = f32[4,6,256]{2,1,0:T(8,128)S(1)} all-gather(f32[1,6,256]{2,1,0:T(8,128)S(1)} %fusion.52), channel_id=3, replica_groups=mesh['groups'=2,'blk_0'=16,'blk_1'=4,'blk_2'=2] {'blk_1'}, dimensions={0}, use_global_device_ids=true | all-gather | bytes 30720 | tf_op jit(solution)/shard_map/all_gather | solution.py:45
  263.8 29.0 %all_gather.22 = f32[64,6,256]{2,1,0:T(8,128)S(1)} all-gather(f32[4,6,256]{2,1,0:T(8,128)S(1)} %all-gather.3), channel_id=1, replica_groups=mesh['groups'=2,'blk_0'=16,'blk_1'=4,'blk_2'=2] {'blk_0'}, dimensions={0}, use_global_device_ids=true | all-gather | bytes 417792 | tf_op jit(solution)/shard_map/all_gather | solution.py:45
  293.0 2.4 all_gather.23
  295.4 0.2 reshape.143
  295.6 0.6 copy.107
  296.2 0.5 reshape.144
  297.0 0.3 copy.109
  297.3 0.3 copy.110
  297.6 66.1 %while.27 = (s32[]{:T(128)}, f32[3,256]{1,0:T(4,128)S(1)}, f32[3,256]{1,0:T(4,128)S(1)}, f32[8,3,4096]{2,1,0:T(4,128)S(1)}, f32[8,3,4096]{2,1,0:T(4,128)S(1)}, /*index=5*/s32[]{:T(128)}, s32[]{:T(128)}, s32[]{}, s32[]{}) while((s32[]{:T(128)}, f32[3,256]{1,0:T(4,128)S(1)}, f32[3,256]{1,0:T(4,128)S(1)}, ...), condition=%wide.region_24.26_spmd.clone, body=%wide.region_20.25_spmd.clone.sunk | while | flops 46139652 | bytes 316555 | solution.py:96
  297.7 8.1 %fusion.69 = (f32[256]{0:T(256)S(1)}, f32[256]{0:T(256)S(1)}, f32[256]{0:T(256)S(1)}) fusion(f32[4096]{0:T(1024)S(1)} %bitcast.126, f32[4096]{0:T(1024)S(1)} %bitcast.129, f32[256]{0:T(256)S(1)} %bitcast.143, f32[4096]{0:T(1024)S(1)} %bitcast.128, f32[256]{0:T(256)S(1)} %bitcast.142, f32[4096]{0:T(1024)S(1)} %bitcast.130, f32[256]{0:T(256)S(1)} %bitcast.141, ...), kind=kLoop, calls=%fused_computation.61.clone.1 | loop fusion | flops 46136576 | bytes 104448 | tf_op jit(solution)/shard_map/while/body/eval_jaxpr/reduce_sum | solution.py:79
  306.0 8.1 %fusion.69 = (f32[256]{0:T(256)S(1)}, f32[256]{0:T(256)S(1)}, f32[256]{0:T(256)S(1)}) fusion(f32[4096]{0:T(1024)S(1)} %bitcast.126, f32[4096]{0:T(1024)S(1)} %bitcast.129, f32[256]{0:T(256)S(1)} %bitcast.143, f32[4096]{0:T(1024)S(1)} %bitcast.128, f32[256]{0:T(256)S(1)} %bitcast.142, f32[4096]{0:T(1024)S(1)} %bitcast.130, f32[256]{0:T(256)S(1)} %bitcast.141, ...), kind=kLoop, calls=%fused_computation.61.clone.1 | loop fusion | flops 46136576 | bytes 104448 | tf_op jit(solution)/shard_map/while/body/eval_jaxpr/reduce_sum | solution.py:79
  314.3 8.1 %fusion.69 = (f32[256]{0:T(256)S(1)}, f32[256]{0:T(256)S(1)}, f32[256]{0:T(256)S(1)}) fusion(f32[4096]{0:T(1024)S(1)} %bitcast.126, f32[4096]{0:T(1024)S(1)} %bitcast.129, f32[256]{0:T(256)S(1)} %bitcast.143, f32[4096]{0:T(1024)S(1)} %bitcast.128, f32[256]{0:T(256)S(1)} %bitcast.142, f32[4096]{0:T(1024)S(1)} %bitcast.130, f32[256]{0:T(256)S(1)} %bitcast.141, ...), kind=kLoop, calls=%fused_computation.61.clone.1 | loop fusion | flops 46136576 | bytes 104448 | tf_op jit(solution)/shard_map/while/body/eval_jaxpr/reduce_sum | solution.py:79
  322.5 8.1 %fusion.69 = (f32[256]{0:T(256)S(1)}, f32[256]{0:T(256)S(1)}, f32[256]{0:T(256)S(1)}) fusion(f32[4096]{0:T(1024)S(1)} %bitcast.126, f32[4096]{0:T(1024)S(1)} %bitcast.129, f32[256]{0:T(256)S(1)} %bitcast.143, f32[4096]{0:T(1024)S(1)} %bitcast.128, f32[256]{0:T(256)S(1)} %bitcast.142, f32[4096]{0:T(1024)S(1)} %bitcast.130, f32[256]{0:T(256)S(1)} %bitcast.141, ...), kind=kLoop, calls=%fused_computation.61.clone.1 | loop fusion | flops 46136576 | bytes 104448 | tf_op jit(solution)/shard_map/while/body/eval_jaxpr/reduce_sum | solution.py:79
  330.8 8.1 %fusion.69 = (f32[256]{0:T(256)S(1)}, f32[256]{0:T(256)S(1)}, f32[256]{0:T(256)S(1)}) fusion(f32[4096]{0:T(1024)S(1)} %bitcast.126, f32[4096]{0:T(1024)S(1)} %bitcast.129, f32[256]{0:T(256)S(1)} %bitcast.143, f32[4096]{0:T(1024)S(1)} %bitcast.128, f32[256]{0:T(256)S(1)} %bitcast.142, f32[4096]{0:T(1024)S(1)} %bitcast.130, f32[256]{0:T(256)S(1)} %bitcast.141, ...), kind=kLoop, calls=%fused_computation.61.clone.1 | loop fusion | flops 46136576 | bytes 104448 | tf_op jit(solution)/shard_map/while/body/eval_jaxpr/reduce_sum | solution.py:79
  339.0 8.1 %fusion.69 = (f32[256]{0:T(256)S(1)}, f32[256]{0:T(256)S(1)}, f32[256]{0:T(256)S(1)}) fusion(f32[4096]{0:T(1024)S(1)} %bitcast.126, f32[4096]{0:T(1024)S(1)} %bitcast.129, f32[256]{0:T(256)S(1)} %bitcast.143, f32[4096]{0:T(1024)S(1)} %bitcast.128, f32[256]{0:T(256)S(1)} %bitcast.142, f32[4096]{0:T(1024)S(1)} %bitcast.130, f32[256]{0:T(256)S(1)} %bitcast.141, ...), kind=kLoop, calls=%fused_computation.61.clone.1 | loop fusion | flops 46136576 | bytes 104448 | tf_op jit(solution)/shard_map/while/body/eval_jaxpr/reduce_sum | solution.py:79
  347.3 8.1 %fusion.69 = (f32[256]{0:T(256)S(1)}, f32[256]{0:T(256)S(1)}, f32[256]{0:T(256)S(1)}) fusion(f32[4096]{0:T(1024)S(1)} %bitcast.126, f32[4096]{0:T(1024)S(1)} %bitcast.129, f32[256]{0:T(256)S(1)} %bitcast.143, f32[4096]{0:T(1024)S(1)} %bitcast.128, f32[256]{0:T(256)S(1)} %bitcast.142, f32[4096]{0:T(1024)S(1)} %bitcast.130, f32[256]{0:T(256)S(1)} %bitcast.141, ...), kind=kLoop, calls=%fused_computation.61.clone.1 | loop fusion | flops 46136576 | bytes 104448 | tf_op jit(solution)/shard_map/while/body/eval_jaxpr/reduce_sum | solution.py:79
  355.6 8.1 %fusion.69 = (f32[256]{0:T(256)S(1)}, f32[256]{0:T(256)S(1)}, f32[256]{0:T(256)S(1)}) fusion(f32[4096]{0:T(1024)S(1)} %bitcast.126, f32[4096]{0:T(1024)S(1)} %bitcast.129, f32[256]{0:T(256)S(1)} %bitcast.143, f32[4096]{0:T(1024)S(1)} %bitcast.128, f32[256]{0:T(256)S(1)} %bitcast.142, f32[4096]{0:T(1024)S(1)} %bitcast.130, f32[256]{0:T(256)S(1)} %bitcast.141, ...), kind=kLoop, calls=%fused_computation.61.clone.1 | loop fusion | flops 46136576 | bytes 104448 | tf_op jit(solution)/shard_map/while/body/eval_jaxpr/reduce_sum | solution.py:79
  364.9 10.8 %gather_fusion.1 = f32[4096,6]{1,0:T(8,128)S(1)} fusion(f32[6,320]{0,1:T(8,128)S(1)} %copy.97, s32[4096]{0:T(1024)S(1)} %broadcast_clamp_fusion), kind=kCustom, calls=%fused_computation.1.clone | custom fusion | bytes 212992 | tf_op jit(solution)/shard_map/jit(_take)/gather | solution.py:128
  375.6 0.7 select_bitcast_fusion
  376.4 1.7 multiply_reduce_fusion.1
  378.1 0.7 multiply_reduce_fusion
  378.9 0.6 multiply_reduce_fusion.4
  379.5 29.5 %all-reduce = (f32[]{:T(128)}, f32[]{:T(128)}, f32[]{:T(128)}) all-reduce(f32[]{:T(128)} %get-tuple-element.191, f32[]{:T(128)} %get-tuple-element.190, f32[]{:T(128)} %get-tuple-element.189), channel_id=1, replica_groups=mesh['groups'=2,'blk_0'=16,'blk_1'=4,'blk_2'=2] {'blk_0'}, use_global_device_ids=true, to_apply=%region_29.31 | all-reduce | flops 3 | bytes 24 | tf_op jit(solution)/shard_map/psum | solution.py:57
  409.0 8.6 %all-reduce.2 = (f32[]{:T(128)}, f32[]{:T(128)}, f32[]{:T(128)}) all-reduce(f32[]{:T(128)} %get-tuple-element.214, f32[]{:T(128)} %get-tuple-element.215, f32[]{:T(128)} %get-tuple-element.216), channel_id=1, replica_groups=mesh['groups'=2,'blk_0'=16,'blk_1'=4,'blk_2'=2] {'blk_1'}, use_global_device_ids=true, to_apply=%region_30.32 | all-reduce | flops 3 | bytes 24 | tf_op jit(solution)/shard_map/psum | solution.py:57
  417.7 3.2 all-reduce.4
  427.1 0.6 multiply_add_fusion
  427.7 0.6 multiply_subtract_fusion
  (86 shorter events, 3.8 us)
Async XLA Ops:
  68.7 118.7 %collective-permute-start = (f32[6,32]{1,0:T(8,128)S(1)}, f32[6,32]{1,0:T(8,128)S(1)}, u32[]{:S(2)}, u32[]{:S(2)}) collective-permute-start(f32[6,32]{1,0:T(8,128)S(1)} %get-tuple-element.261), channel_id=1, source_target_pairs={{0,1},{1,2},{2,3},{3,4},{4,5},{5,6},{6,7},{7,8},{8,9},{9,10},{10,1... | collective-permute-start | bytes 2312 | tf_op jit(solution)/shard_map/ppermute | solution.py:27
  69.0 118.5 %collective-permute-start.1 = (f32[6,32]{1,0:T(8,128)S(1)}, f32[6,32]{1,0:T(8,128)S(1)}, u32[]{:S(2)}, u32[]{:S(2)}) collective-permute-start(f32[6,32]{1,0:T(8,128)S(1)} %get-tuple-element.262), channel_id=1, source_target_pairs={{1,0},{2,1},{3,2},{4,3},{5,4},{6,5},{7,6},{8,7},{9,8},{10,9},{11,1... | collective-permute-start | bytes 2312 | tf_op jit(solution)/shard_map/ppermute | solution.py:29
  120.3 0.7 copy-start
  121.0 66.1 %copy-start.2 = (s32[16,256]{1,0:T(8,128)S(1)}, s32[16,256]{1,0:T(8,128)}, u32[]{:S(2)}) copy-start(s32[16,256]{1,0:T(8,128)} %param.12) | copy-start | bytes 49156
  199.2 1.8 copy-start.3
  201.0 0.8 copy-start.1
  246.5 118.1 %collective-permute-start.2 = (f32[6,32]{1,0:T(8,128)S(1)}, f32[6,32]{1,0:T(8,128)S(1)}, u32[]{:S(2)}, u32[]{:S(2)}) collective-permute-start(f32[6,32]{1,0:T(8,128)S(1)} %get-tuple-element.259), channel_id=1, source_target_pairs={{0,1},{1,2},{2,3},{3,4},{4,5},{5,6},{6,7},{7,8},{8,9},{9,10},{10,1... | collective-permute-start | bytes 2312 | tf_op jit(solution)/shard_map/ppermute | solution.py:27
  246.8 117.8 %collective-permute-start.3 = (f32[6,32]{1,0:T(8,128)S(1)}, f32[6,32]{1,0:T(8,128)S(1)}, u32[]{:S(2)}, u32[]{:S(2)}) collective-permute-start(f32[6,32]{1,0:T(8,128)S(1)} %get-tuple-element.260), channel_id=1, source_target_pairs={{1,0},{2,1},{3,2},{4,3},{5,4},{6,5},{7,6},{8,7},{9,8},{10,9},{11,1... | collective-permute-start | bytes 2312 | tf_op jit(solution)/shard_map/ppermute | solution.py:29
where the time goes:
time: 430 us; the launch traced here: 428 us
  blocking collectives  234 us (54%)
  other arithmetic  144 us (33%)
  local copies, waits for them, and re-layouts  28.6 us (7%)
  between operations  10.7 us (2%)
  starting transfers between devices  10.3 us (2%)
    psum x9, blocking collectives, one_axis_at_a_time(): return functools.reduce(lax.psum, axes, array)  147 us
    reduce_sum x16, other arithmetic, far_tile(): out_x = jnp.sum(coef_a * col_vec[0][None, :] + weighted * dx, axis=1)  130 us
    all_gather x6, blocking collectives, stacked_from(): tiles = lax.all_gather(tiles, axes[k], axis=0, tiled=True)  87 us
    gather x2, local copies, waits for them, and re-layouts, on_device(): picked = jnp.take(extended, local_slot, axis=1)  21.6 us
    ppermute x2, starting transfers between devices, extended_2(): lax.ppermute(head, axis, [((i + 1) % count, i) for i in range(count)])  9.8 us
  transfers between devices with their start and end apart: 4, of which 0 were waited for; matrix products, arithmetic and copies ran while one was open for 32% of the time, Pallas kernels for 0%

commit v1 on v0

v1 whole, which is shorter than its diff:
```python
import functools
import math

import jax
import jax.numpy as jnp
from jax import lax
from jax.experimental import pallas as pl
from jax.experimental.pallas import tpu as pltpu
from jax.sharding import Mesh
from jax.sharding import PartitionSpec as P

REACH = 32
AXES = ("blk_0", "blk_1", "blk_2")
GROUPS_BLK = ("groups",) + AXES
MESH = pl.DeviceIdType.MESH
F32, BF16 = jnp.float32, jnp.bfloat16

SOFT = 0.0001
EPS = 1e-06
G = math.sqrt(0.75)
EDGE = 2.0 * G
FACT_A = 0.375 * G
FACT_B = 1.125 * G

RING = 12
CHUNK = 32


def hop(k):
    return ((k + 1) // 2) * (2 * (k % 2) - 1)


def total_of(x):
    return jnp.sum(jnp.sum(x, axis=1, keepdims=True), axis=0, keepdims=True)


def limbs(x, count):
    parts = []
    for k in range(count):
        part = x.astype(BF16)
        parts.append(part)
        if k < count - 1:
            x = x - part.astype(F32)
    return parts


def kernel(
    sizes, rows,
    pos_ref, rhs_ref, nbr_ref, cnt_ref,
    sol_ref, res_ref, a_hbm,
    blk, vec, red_c, red_x, red_z,
    keep_b, ring, stage_0, stage_1, wst_0, wst_1, acc, mult, centre, scale, lub, tot,
    recv_1, send_z1, send_x1, send_c1,
    recv_2, send_z2, send_x2, send_c2,
    recv_3, send_3, ring_out, ring_in,
):
    nz, nx, nc = sizes
    span = nx * nc
    tiles = nz * span
    pairs = tiles // 2
    ppg = span // 2
    zi, xi, ci = (lax.axis_index(a) for a in AXES)
    me = (zi * nx + xi) * nc + ci
    total = tiles * rows
    zoff = lambda k: (zi + hop(k) + nz) % nz
    xoff = lambda k: (xi + hop(k) + nx) % nx
    index = lambda z, x, c: (z * nx + x) * nc + c
    plus = nz // 2

    def source(t):
        group, inner = t // span, t % span
        return index(zoff(group), xoff(inner // nc), (ci + inner % nc) % nc)

    barrier = pltpu.get_barrier_semaphore()
    near = []
    for step in sorted({1 % nz, nz - 1} - {0}):
        near.append({"blk_0": (zi + step) % nz})
    for step in range(1, nx):
        near.append({"blk_1": (xi + step) % nx})
    for step in range(1, nc):
        near.append({"blk_2": (ci + step) % nc})
    for peer in near:
        pl.semaphore_signal(barrier, inc=1, device_id=peer, device_id_type=MESH)

    ones = jnp.ones((1, rows), F32)
    blk[me] = jnp.concatenate(
        [pos_ref[...], rhs_ref[...], ones, jnp.zeros((1, rows), F32)], axis=0
    )
    middle = jnp.sum(pos_ref[...], axis=1, keepdims=True) * (1.0 / rows)
    centre[...] = jnp.concatenate(
        [jnp.broadcast_to(middle, (3, rows)), jnp.zeros((5, rows), F32)], axis=0
    )
    line = lax.broadcasted_iota(jnp.int32, (8, rows), 0)
    scale[...] = jnp.where(line < 3, G, 1.0).astype(F32)
    own = me * rows + lax.broadcasted_iota(jnp.int32, nbr_ref.shape, 1)
    slot = lax.broadcasted_iota(jnp.int32, nbr_ref.shape, 0)
    offset = (nbr_ref[...] - own + (REACH + total)) % total
    offset = jnp.where(slot < cnt_ref[...], offset, -1)
    for o in range(2 * REACH + 1):
        mult[o : o + 1, :] = jnp.sum(
            jnp.where(offset == o, 1.0, 0.0), axis=0, keepdims=True
        )
    mult[2 * REACH + 1 :, :] = jnp.zeros((mult.shape[0] - 2 * REACH - 1, rows), F32)
    acc[...] = jnp.zeros(acc.shape, F32)

    pl.semaphore_wait(barrier, len(near))

    def copy(buf, s, send, recv, peer):
        return pltpu.make_async_remote_copy(
            src_ref=buf.at[s], dst_ref=buf.at[s], send_sem=send, recv_sem=recv.at[s],
            device_id=peer, device_id_type=MESH,
        )

    here = {"blk_0": zi}
    up = {"blk_0": (zi + 1) % nz}
    down = {"blk_0": (zi + nz - 1) % nz}

    def x_copies(buf, s, send, recv, g):
        return [
            copy(buf, s, send.at[g, k - 1], recv, {"blk_1": xoff(k)}) for k in range(1, nx)
        ]

    def c_copies(buf, s, send, recv, g, k):
        return [copy(buf, s, send.at[g, k], recv, {"blk_2": (ci + 1) % nc})]

    def arrived(buf, s, send, recv):
        copy(buf, s, send, recv, up).wait_recv()

    def at_z(g):
        return index(zoff(g), xi, ci)

    def spread_z(buf, send_x, send_c, recv, g):
        for c in x_copies(buf, at_z(g), send_x, recv, g):
            c.start()
        for c in c_copies(buf, at_z(g), send_c, recv, g, 0):
            c.start()

    def spread_x(buf, send_x, send_c, recv, g):
        for k in range(1, nx):
            s = index(zoff(g), xoff(k), ci)
            arrived(buf, s, send_x.at[g, 0], recv)
            for c in c_copies(buf, s, send_c, recv, g, k):
                c.start()

    def wait_c(buf, send_c, recv, g):
        for k in range(nx):
            s = index(zoff(g), xoff(k), (ci + 1) % nc)
            arrived(buf, s, send_c.at[g, 0], recv)

    def relay_z(g):
        s = at_z(g)
        arrived(blk, s, send_z1.at[0], recv_1)
        j = (g + 1) // 2

        @pl.when((g % 2 == 1) & (j < plus))
        def _():
            copy(blk, s, send_z1.at[g + 1], recv_1, down).start()

        @pl.when((g % 2 == 0) & (j < nz - 1 - plus))
        def _():
            copy(blk, s, send_z1.at[g + 1], recv_1, up).start()

        spread_z(blk, send_x1, send_c1, recv_1, g)

    def finish_sends(buf, send_x, send_c, recv):
        def body(g, _):
            s = at_z(g)
            for c in x_copies(buf, s, send_x, recv, g):
                c.wait_send()
            for k in range(nx):
                for c in c_copies(buf, s, send_c, recv, g, k):
                    c.wait_send()
            return 0

        lax.fori_loop(0, nz, body, 0)

    own_row = (blk[me] - centre[...]) * scale[...]
    xs = [own_row[c : c + 1, :] for c in range(3)]

    def centred(s):
        return (blk[s] - centre[...]) * scale[...]

    def weights(block, vectors, out):
        along = sum(block[c : c + 1, :] * vectors[c] for c in range(3))
        columns = [
            jnp.broadcast_to(v, (8, rows)) * block for v in vectors + [along]
        ]
        for k, part in enumerate(limbs(jnp.concatenate(columns, axis=0), 3)):
            out[32 * k : 32 * (k + 1), :] = part

    def coefficients(t, half, stage, out, slot, masked):
        s = source(t)
        block = centred(s)
        raw = blk[s]
        weights(block, [raw[3 + c : 4 + c, :] for c in range(3)], out)
        turned = block.T
        for j in range(rows // CHUNK):
            part = slice(j * CHUNK, (j + 1) * CHUNK)
            dx, dy, dz = (turned[part, c : c + 1] - xs[c] for c in range(3))
            square = (dx * dx + dy * dy) + (dz * dz + SOFT * 0.75)
            q = lax.rsqrt(square)
            q_far = jnp.minimum(q, 1.0 / EDGE)
            q2 = q_far * q_far
            a = q_far * (q2 + 2.0) + jnp.maximum(EDGE - square * q, 0.0)
            b = (q * q2) * (2.0 / 3.0 - q2)
            if masked:
                first = lax.broadcasted_iota(jnp.int32, b.shape, 0) + j * CHUNK
                second = lax.broadcasted_iota(jnp.int32, b.shape, 1)
                b = jnp.where(first == second, 0.0, b)
            for k, piece in enumerate(limbs(a, 2)):
                stage[k, part, :] = piece
                ring[slot, 2 * half + k, part, :] = piece
            for k, piece in enumerate(limbs(b, 3)):
                stage[2 + k, part, :] = piece
                keep_b[t, k, part, :] = piece

    def dot(w, m):
        return jnp.dot(w, m, preferred_element_type=F32)

    def product(w, a_parts, b_parts):
        acc[0] += dot(w, a_parts[0]) + dot(w, a_parts[1])
        acc[1] += dot(w, b_parts[0]) + dot(w, b_parts[1]) + dot(w, b_parts[2])

    def staged(stage, out):
        product(out[...], [stage[k] for k in range(2)], [stage[2 + k] for k in range(3)])

    def ring_write(p):
        return pltpu.make_async_copy(ring.at[p % RING], a_hbm.at[p], ring_out.at[p % RING])

    def ring_read(p):
        return pltpu.make_async_copy(a_hbm.at[p], ring.at[p % RING], ring_in.at[p % RING])

    copy(blk, me, send_z1.at[0], recv_1, up).start()
    copy(blk, me, send_z1.at[1], recv_1, down).start()
    spread_z(blk, send_x1, send_c1, recv_1, 0)

    def pair(p, masked):
        slot = p % RING
        coefficients(2 * p, 0, stage_0, wst_0, slot, masked)
        staged(stage_0, wst_0)
        coefficients(2 * p + 1, 1, stage_1, wst_1, slot, False)

    coefficients(0, 0, stage_0, wst_0, 0, True)
    staged(stage_0, wst_0)
    spread_x(blk, send_x1, send_c1, recv_1, 0)
    wait_c(blk, send_c1, recv_1, 0)
    relay_z(1)
    coefficients(1, 1, stage_1, wst_1, 0, False)

    def first(p, _):
        g = p // ppg

        @pl.when((p % ppg == 0) & (g + 1 < nz))
        def _():
            relay_z(g + 1)

        @pl.when(p % ppg == 0)
        def _():
            spread_x(blk, send_x1, send_c1, recv_1, g)
            wait_c(blk, send_c1, recv_1, g)

        @pl.when(p >= RING)
        def _():
            ring_write(p - RING).wait()

        staged(stage_1, wst_1)
        coefficients(2 * p, 0, stage_0, wst_0, p % RING, False)
        staged(stage_0, wst_0)
        coefficients(2 * p + 1, 1, stage_1, wst_1, p % RING, False)
        ring_write(p - 1).start()
        return 0

    lax.fori_loop(1, pairs, first, 0)
    staged(stage_1, wst_1)

    def sums():
        out = []
        for k in range(2):
            parts = acc[k]
            out.append((parts[0:32] + parts[32:64]) + parts[64:96])
        a, b = out
        row = lambda m, r: m[r : r + 1, :]
        bv = [row(b, 8 * c + 6) for c in range(3)]
        along = sum(xs[c] * bv[c] for c in range(3)) - row(b, 30)
        far = []
        for k in range(3):
            cross = sum(xs[c] * row(b, 8 * c + k) for c in range(3))
            far.append(
                FACT_A * row(a, 8 * k + 6)
                + FACT_B * ((xs[k] * along - cross) + row(b, 24 + k))
            )
        return far

    before, after = (me + tiles - 1) % tiles, (me + 1) % tiles

    def lubricated(rows_of):
        def six(s):
            return jnp.concatenate([blk[s][0:3, :]] + rows_of(s), axis=0)

        wide = jnp.concatenate([six(before), six(me), six(after)], axis=1)
        mine = six(me)
        for o in range(2 * REACH + 1):
            begin = rows + o - REACH
            delta = mine - wide[:, begin : begin + rows]
            for k in range(6):
                lub[k, o : o + 1, :] = delta[k : k + 1, :]
        for k in range(6):
            lub[k, 2 * REACH + 1 :, :] = jnp.zeros((lub.shape[1] - 2 * REACH - 1, rows), F32)
        d = [lub[k] for k in range(3)]
        e = [lub[3 + k] for k in range(3)]
        square = d[0] * d[0] + d[1] * d[1] + d[2] * d[2] + SOFT
        dist = jnp.sqrt(square)
        strength = mult[...] / ((0.5 + jnp.abs(dist - 2.0)) * square)
        force = strength * (d[0] * e[0] + d[1] * e[1] + d[2] * e[2])
        return [jnp.sum(force * d[k], axis=0, keepdims=True) for k in range(3)]

    rhs = [rhs_ref[k : k + 1, :] for k in range(3)]
    far = sums()
    near_part = lubricated(lambda s: [blk[s][3:6, :]])
    work = [far[k] + near_part[k] for k in range(3)]
    inner = lambda u, v: total_of(u[0] * v[0] + u[1] * v[1] + u[2] * v[2])
    lane = lax.broadcasted_iota(jnp.int32, (1, rows), 1)

    def packed(values):
        line = jnp.zeros((1, rows), F32)
        for k, value in enumerate(values):
            line = jnp.where(lane == k, value, line)
        return line

    def unpacked(line, count):
        return [
            jnp.sum(jnp.where(lane[:, : line.shape[1]] == k, line, 0.0), axis=1, keepdims=True)
            for k in range(count)
        ]

    vec[me] = jnp.concatenate(
        work + [packed([inner(rhs, rhs), inner(work, rhs), inner(work, work)])], axis=0
    )

    def last_writes(p, _):
        ring_write(p).wait()
        return 0

    ring_write(pairs - 1).start()
    lax.fori_loop(max(pairs - RING, 0), pairs, last_writes, 0)
    for p in range(min(RING, pairs)):
        ring_read(p).start()

    def z_copy(k):
        return copy(vec, me, send_z2.at[k], recv_2, {"blk_0": zoff(k)})

    def z_start(k, _):
        z_copy(k).start()
        return 0

    lax.fori_loop(1, nz, z_start, 0)
    spread_z(vec, send_x2, send_c2, recv_2, 0)
    acc[...] = jnp.zeros(acc.shape, F32)
    tot[...] = jnp.zeros(tot.shape, F32)

    LOOK_Z, LOOK_X = 4, 2

    def far_stage(g):
        arrived(vec, at_z(g), send_z2.at[0], recv_2)
        spread_z(vec, send_x2, send_c2, recv_2, g)

    def mid_stage(g):
        spread_x(vec, send_x2, send_c2, recv_2, g)

    def group(g, _):
        @pl.when(g + LOOK_Z < nz)
        def _():
            far_stage(g + LOOK_Z)

        @pl.when(g + LOOK_X < nz)
        def _():
            mid_stage(g + LOOK_X)

        wait_c(vec, send_c2, recv_2, g)

        def second(i, _):
            p = g * ppg + i
            ring_read(p).wait()
            for half in range(2):
                t = 2 * p + half
                s = source(t)
                v = vec[s]
                tot[...] += v
                out = wst_0 if half == 0 else wst_1
                weights(centred(s), [v[c : c + 1, :] for c in range(3)], out)
                product(
                    out[...],
                    [ring[p % RING, 2 * half + k] for k in range(2)],
                    [keep_b[t, k] for k in range(3)],
                )

            @pl.when(p + RING < pairs)
            def _():
                ring_read(p + RING).start()

            return 0

        lax.fori_loop(0, ppg, second, 0)
        return 0

    mid_stage(0)
    for g in range(1, min(LOOK_Z, nz)):
        far_stage(g)
    for g in range(1, min(LOOK_X, nz)):
        mid_stage(g)
    lax.fori_loop(0, nz, group, 0)

    far = sums()
    near_part = lubricated(lambda s: [vec[s][0:3, :]])
    again = [far[k] + near_part[k] for k in range(3)]

    rr, wr, ww = unpacked(tot[3:4, :], 3)
    beta = jnp.sqrt(rr + EPS)
    image_0 = [work[k] / beta for k in range(3)]
    v_0 = [rhs[k] / beta for k in range(3)]
    h_00 = wr / (beta * beta)
    h_10 = jnp.sqrt(ww / (beta * beta) - h_00 * h_00 + EPS)
    v_1 = [(image_0[k] - h_00 * v_0[k]) / h_10 for k in range(3)]
    image_1 = [(again[k] / beta - h_00 * image_0[k]) / h_10 for k in range(3)]
    line = packed([inner(image_1, v_0), inner(image_1, v_1), inner(image_1, image_1)])[:, :128]

    def summed(buf, mine, count, peers, first_sem):
        buf[mine] = line
        copies = [
            pltpu.make_async_remote_copy(
                src_ref=buf.at[mine], dst_ref=buf.at[mine],
                send_sem=send_3.at[first_sem + k], recv_sem=recv_3.at[first_sem + mine],
                device_id=peer, device_id_type=MESH,
            )
            for k, peer in enumerate(peers)
        ]
        for c in copies:
            c.start()
        return copies

    def collected(buf, mine, count, copies, others, first_sem):
        for k, other in enumerate(others):
            pltpu.make_async_remote_copy(
                src_ref=buf.at[mine], dst_ref=buf.at[other],
                send_sem=send_3.at[first_sem + k], recv_sem=recv_3.at[first_sem + other],
                device_id=up, device_id_type=MESH,
            ).wait_recv()
        out = buf[0]
        for k in range(1, count):
            out = out + buf[k]
        for c in copies:
            c.wait_send()
        return out

    base = 0
    for buf, mine, count, name in (
        (red_c, ci, nc, "blk_2"), (red_x, xi, nx, "blk_1"), (red_z, zi, nz, "blk_0")
    ):
        others = [(mine + k) % count for k in range(1, count)]
        copies = summed(buf, mine, count, [{name: o} for o in others], base)
        line = collected(buf, mine, count, copies, others, base)
        base += count
    h_01, h_11, squares = unpacked(line, 3)
    h_21 = jnp.sqrt(squares - h_01 * h_01 - h_11 * h_11 + EPS)

    rho_0 = jnp.sqrt(h_00 * h_00 + h_10 * h_10)
    c_0, s_0 = h_00 / rho_0, h_10 / rho_0
    g_1 = -s_0 * beta
    g_0 = c_0 * beta
    r_01 = c_0 * h_01 + s_0 * h_11
    r_11 = c_0 * h_11 - s_0 * h_01
    rho_1 = jnp.sqrt(r_11 * r_11 + h_21 * h_21)
    g_1 = (r_11 / rho_1) * g_1
    y_1 = g_1 / rho_1
    y_0 = (g_0 - r_01 * y_1) / rho_0
    for k in range(3):
        sol_ref[k : k + 1, :] = y_0 * v_0[k] + y_1 * v_1[k]
        res_ref[k : k + 1, :] = rhs[k] - y_0 * image_0[k] - y_1 * image_1[k]

    def z_done(k, _):
        z_copy(k).wait_send()
        return 0

    lax.fori_loop(1, nz, z_done, 0)
    copy(blk, me, send_z1.at[0], recv_1, up).wait_send()
    copy(blk, me, send_z1.at[1], recv_1, down).wait_send()

    def relay_done(g, _):
        j = (g + 1) // 2

        @pl.when(((g % 2 == 1) & (j < plus)) | ((g % 2 == 0) & (j < nz - 1 - plus)))
        def _():
            copy(blk, me, send_z1.at[g + 1], recv_1, up).wait_send()

        return 0

    lax.fori_loop(1, nz, relay_done, 0)
    finish_sends(blk, send_x1, send_c1, recv_1)
    finish_sends(vec, send_x2, send_c2, recv_2)


def on_device(positions, right_side, neighbours, counts):
    rows = positions.shape[1]
    sizes = nz, nx, nc = tuple(lax.axis_size(a) for a in AXES)
    tiles = nz * nx * nc
    slots = 8 * -(-(2 * REACH + 1) // 8)
    vmem = pl.BlockSpec(memory_space=pltpu.VMEM)
    dma = pltpu.SemaphoreType.DMA
    small = jax.ShapeDtypeStruct((3, rows), F32)
    gather_sems = [dma((tiles,)), dma((nz + 2,)), dma((nz, max(nx - 1, 1))), dma((nz, nx))]
    out = pl.pallas_call(
        functools.partial(kernel, sizes, rows),
        out_shape=(small, small, jax.ShapeDtypeStruct((tiles // 2, 4, rows, rows), BF16)),
        in_specs=[vmem] * 4,
        out_specs=(vmem, vmem, pl.BlockSpec(memory_space=pltpu.HBM)),
        scratch_shapes=[
            pltpu.VMEM((tiles, 8, rows), F32),
            pltpu.VMEM((tiles, 4, rows), F32),
            pltpu.VMEM((nc, 1, 128), F32),
            pltpu.VMEM((nx, 1, 128), F32),
            pltpu.VMEM((nz, 1, 128), F32),
            pltpu.VMEM((tiles, 3, rows, rows), BF16),
            pltpu.VMEM((RING, 4, rows, rows), BF16),
            pltpu.VMEM((5, rows, rows), BF16),
            pltpu.VMEM((5, rows, rows), BF16),
            pltpu.VMEM((96, rows), BF16),
            pltpu.VMEM((96, rows), BF16),
            pltpu.VMEM((2, 96, rows), F32),
            pltpu.VMEM((slots, rows), F32),
            pltpu.VMEM((8, rows), F32),
            pltpu.VMEM((8, rows), F32),
            pltpu.VMEM((6, slots, rows), F32),
            pltpu.VMEM((4, rows), F32),
        ]
        + gather_sems * 2
        + [dma((nz + nx + nc,)), dma((nz + nx + nc,)), dma((RING,)), dma((RING,))],
        compiler_params=pltpu.CompilerParams(
            collective_id=0, has_side_effects=True, vmem_limit_bytes=67043328
        ),
    )(positions, right_side, neighbours, counts[None, :])
    return out[0], out[1]


def solution(mesh):
    torus = Mesh(mesh.devices.reshape(mesh.shape["groups"], 16, 4, 2), GROUPS_BLK)
    placed = (P(None, GROUPS_BLK), P(None, GROUPS_BLK), P(None, GROUPS_BLK), P(GROUPS_BLK))
    return jax.shard_map(
        on_device,
        mesh=torus,
        in_specs=placed,
        out_specs=(P(None, GROUPS_BLK), P(None, GROUPS_BLK)),
        check_vma=False,
    )
```

time: 430 us -> 157 us (0.37)
  blocking collectives: 234 us -> 0 us
  Pallas kernels: 0 us -> 154 us
  other arithmetic: 144 us -> 0 us
  local copies, waits for them, and re-layouts: 28.6 us -> 2.55 us
  starting transfers between devices: 10.3 us -> 0 us
  between operations: 10.7 us -> 0.64 us
    pallas_call x0 -> x1, Pallas kernels: none -> 154 us  [on_device(): pl.pallas_call(functools.partial(kernel, sizes, rows), out_shape=(small,...]
    psum x9 -> x0, blocking collectives: 147 us -> none  [one_axis_at_a_time(): return functools.reduce(lax.psum, axes, array)]
    reduce_sum x23 -> x0, other arithmetic: 137 us -> none  [the longest x16 130 us: far_tile(): out_x = jnp.sum(coef_a * col_vec[0][None, :] + weighted * dx, axis=1)]
    all_gather x6 -> x0, blocking collectives: 87 us -> none  [stacked_from(): tiles = lax.all_gather(tiles, axes[k], axis=0, tiled=True)]
    gather x2 -> x0, local copies, waits for them, and re-layouts: 21.6 us -> none  [on_device(): picked = jnp.take(extended, local_slot, axis=1)]
    ppermute x4 -> x0, starting transfers between devices: 10.3 us -> none  [the longest x2 9.8 us: extended_2(): lax.ppermute(head, axis, [((i + 1) % count, i) for i in range(count)])]
  transfers between devices with their start and end apart: 4 -> 0, of which waited for: 0 -> 0; matrix products, arithmetic and copies ran while one was open for 32% -> 0% of each run, Pallas kernels for 0% -> 0%
where the time goes in v1:
time: 157 us
  Pallas kernels  154 us (98%)
  local copies, waits for them, and re-layouts  2.55 us (2%)
    pallas_call x1, Pallas kernels, on_device(): pl.pallas_call(functools.partial(kernel, sizes, rows), out_shape=(small,...  154 us

profile of v1, /device:TPU:40, one launch (start us, length us, event | category | flops | bytes accessed | tf_op | source)
XLA Modules:
  0.0 157.2 jit_solution(16064324394887693231)
XLA Ops:
  0.6 154.0 %shard_map.59 = (f32[3,256]{1,0:T(4,128)}, f32[3,256]{1,0:T(4,128)}, bf16[64,4,256,256]{3,2,1,0:T(8,128)(2,1)}) custom-call(f32[3,256]{1,0:T(4,128)} %pos_ref.1, f32[3,256]{1,0:T(4,128)} %rhs_ref.1, s32[16,256]{1,0:T(8,128)} %nbr_ref.1, s32[1,256]{1,0:T(1,128)} %bitcast.1), custom_call_target="tpu_custom_call" | custom-call | tf_op jit(solution)/shard_map/pallas_call | solution.py:511
  154.6 1.3 copy.8
  155.9 1.3 copy.9

commit v2 on v1

v2 whole, which is shorter than its diff:
```python
import functools
import math

import jax
import jax.numpy as jnp
from jax import lax
from jax.experimental import pallas as pl
from jax.experimental.pallas import tpu as pltpu
from jax.sharding import Mesh
from jax.sharding import PartitionSpec as P

REACH = 32
AXES = ("blk_0", "blk_1", "blk_2")
GROUPS_BLK = ("groups",) + AXES
MESH = pl.DeviceIdType.MESH
F32, BF16 = jnp.float32, jnp.bfloat16

SOFT = 0.0001
EPS = 1e-06
G = math.sqrt(0.75)
EDGE = 2.0 * G
FACT_A = 0.375 * G
FACT_B = 1.125 * G

RING = 4
CHUNK = 32
LOOK_Z, LOOK_X = 6, 2


def hop(k):
    return lax.div(k + 1, 2) * (2 * lax.rem(k, 2) - 1)


def total_of(x):
    return jnp.sum(jnp.sum(x, axis=1, keepdims=True), axis=0, keepdims=True)


def limbs(x, count):
    parts = []
    for k in range(count):
        part = x.astype(BF16)
        parts.append(part)
        if k < count - 1:
            x = x - part.astype(F32)
    return parts


def kernel(
    sizes, rows,
    pos_ref, rhs_ref, nbr_ref, cnt_ref,
    out_ref, a_hbm,
    blk, vec, red_c, red_x, red_z,
    keep_b, ring, stage_0, stage_1, wst_0, wst_1, acc, mult, centre, scale, lub, tot,
    recv_1, core_1, send_z1, send_x1, send_c1,
    recv_2, core_2, send_z2, send_x2, send_c2,
    recv_3, send_3, ring_out, ring_in,
):
    nz, nx, nc = sizes
    span = nx * nc
    tiles = nz * span
    zi, xi, ci = (lax.axis_index(a) for a in AXES)
    total = tiles * rows
    order = (zi * nx + xi) * nc + ci
    zat = lambda k: lax.rem(zi + hop(k) + nz, nz)
    xat = [lax.rem(xi + k, nx) for k in range(nx)]
    cat = [lax.rem(ci + k, nc) for k in range(nc)]
    at = lambda z, x, c: (z * nc + c) * nx + x
    me = at(zi, xi, ci)
    within = [cat[d] * nx + xat[k] for d in range(nc) for k in range(nx)]
    plus = nz // 2
    stages, wsts = (stage_0, stage_1), (wst_0, wst_1)

    barrier = pltpu.get_barrier_semaphore()
    near = []
    for step in sorted({1 % nz, nz - 1} - {0}):
        near.append({"blk_0": lax.rem(zi + step, nz)})
    near += [{"blk_1": x} for x in xat[1:]] + [{"blk_2": c} for c in cat[1:]]
    for peer in near:
        pl.semaphore_signal(barrier, inc=1, device_id=peer, device_id_type=MESH)

    ones = jnp.ones((1, rows), F32)
    blk[me] = jnp.concatenate(
        [pos_ref[...], rhs_ref[...], ones, jnp.zeros((1, rows), F32)], axis=0
    )
    middle = jnp.sum(pos_ref[...], axis=1, keepdims=True) * (1.0 / rows)
    centre[...] = jnp.concatenate(
        [jnp.broadcast_to(middle, (3, rows)), jnp.zeros((5, rows), F32)], axis=0
    )
    line = lax.broadcasted_iota(jnp.int32, (8, rows), 0)
    scale[...] = jnp.where(line < 3, G, 1.0).astype(F32)
    acc[...] = jnp.zeros(acc.shape, F32)
    pl.semaphore_wait(barrier, len(near))

    def copy(buf, s, send, recv, peer):
        return pltpu.make_async_remote_copy(
            src_ref=buf.at[s], dst_ref=buf.at[s], send_sem=send, recv_sem=recv,
            device_id=peer, device_id_type=MESH,
        )

    up = {"blk_0": lax.rem(zi + 1, nz)}
    down = {"blk_0": lax.rem(zi + nz - 1, nz)}
    beside = {"blk_2": cat[nc - 1]}

    def x_copies(buf, s, send, recv, g):
        return [
            copy(buf, s, send.at[g, k - 1], recv.at[s], {"blk_1": xat[k]}) for k in range(1, nx)
        ]

    def c_copy(buf, send, core, g, z, c):
        return copy(buf, pl.ds((z * nc + c) * nx, nx), send.at[g], core.at[z], beside)

    def z_stage(buf, send_x, recv, g, z):
        s = at(z, xi, ci)
        copy(buf, s, send_x.at[g, 0], recv.at[s], up).wait_recv()
        for c in x_copies(buf, s, send_x, recv, g):
            c.start()

    def x_stage(buf, send_x, send_c, recv, core, g, z):
        for k in range(1, nx):
            s = at(z, xat[k], ci)
            copy(buf, s, send_x.at[g, 0], recv.at[s], up).wait_recv()
        c_copy(buf, send_c, core, g, z, ci).start()

    def c_stage(buf, send_c, core, g, z):
        c_copy(buf, send_c, core, g, z, cat[nc - 1]).wait_recv()

    def relay(g, z):
        s = at(z, xi, ci)
        copy(blk, s, send_z1.at[0], recv_1.at[s], up).wait_recv()
        j, odd = lax.div(g + 1, 2), lax.rem(g, 2)

        @pl.when((odd == 1) & (j < plus))
        def _():
            copy(blk, s, send_z1.at[g + 1], recv_1.at[s], down).start()

        @pl.when((odd == 0) & (j < nz - 1 - plus))
        def _():
            copy(blk, s, send_z1.at[g + 1], recv_1.at[s], up).start()

        for c in x_copies(blk, s, send_x1, recv_1, g):
            c.start()

    def finish_sends(buf, send_x, send_c, recv, core):
        def body(g, _):
            for c in x_copies(buf, me, send_x, recv, g):
                c.wait_send()
            c_copy(buf, send_c, core, g, g, ci).wait_send()
            return 0

        lax.fori_loop(0, nz, body, 0)

    own_row = (blk[me] - centre[...]) * scale[...]
    xs = [own_row[c : c + 1, :] for c in range(3)]

    def centred(s):
        return (blk[s] - centre[...]) * scale[...]

    def weights(block, vectors, out):
        along = sum(block[c : c + 1, :] * vectors[c] for c in range(3))
        columns = [
            jnp.broadcast_to(v, (8, rows)) * block for v in vectors + [along]
        ]
        for k, part in enumerate(limbs(jnp.concatenate(columns, axis=0), 3)):
            out[32 * k : 32 * (k + 1), :] = part

    def coefficients(g, slot, n, s, masked):
        stage, t = stages[n % 2], g * span + n
        block = centred(s)
        raw = blk[s]
        weights(block, [raw[3 + c : 4 + c, :] for c in range(3)], wsts[n % 2])
        turned = block.T
        for j in range(rows // CHUNK):
            part = slice(j * CHUNK, (j + 1) * CHUNK)
            dx, dy, dz = (turned[part, c : c + 1] - xs[c] for c in range(3))
            square = (dx * dx + dy * dy) + (dz * dz + SOFT * 0.75)
            q = lax.rsqrt(square)
            q_far = jnp.minimum(q, 1.0 / EDGE)
            q2 = q_far * q_far
            a = q_far * (q2 + 2.0) + jnp.maximum(EDGE - square * q, 0.0)
            b = (q * q2) * (2.0 / 3.0 - q2)
            if masked:
                first = lax.broadcasted_iota(jnp.int32, b.shape, 0) + j * CHUNK
                second = lax.broadcasted_iota(jnp.int32, b.shape, 1)
                b = jnp.where(first == second, 0.0, b)
            for k, piece in enumerate(limbs(a, 2)):
                stage[k, part, :] = piece
                ring[slot, 2 * n + k, part, :] = piece
            for k, piece in enumerate(limbs(b, 3)):
                stage[2 + k, part, :] = piece
                keep_b[t, k, part, :] = piece

    def dot(w, m):
        return jnp.dot(w, m, preferred_element_type=F32)

    def staged(n):
        stage, w = stages[n % 2], wsts[n % 2][...]
        acc[0] += dot(w, stage[0]) + dot(w, stage[1])
        acc[1] += dot(w, stage[2]) + dot(w, stage[3]) + dot(w, stage[4])

    def ring_write(g):
        slot = lax.rem(g, RING)
        return pltpu.make_async_copy(ring.at[slot], a_hbm.at[g], ring_out.at[slot])

    def ring_read(g):
        slot = lax.rem(g, RING)
        return pltpu.make_async_copy(a_hbm.at[g], ring.at[slot], ring_in.at[slot])

    copy(blk, me, send_z1.at[0], recv_1.at[me], up).start()
    copy(blk, me, send_z1.at[1], recv_1.at[me], down).start()
    for c in x_copies(blk, me, send_x1, recv_1, 0):
        c.start()
    coefficients(0, 0, 0, me, True)

    own = order * rows + lax.broadcasted_iota(jnp.int32, nbr_ref.shape, 1)
    rank = lax.broadcasted_iota(jnp.int32, nbr_ref.shape, 0)
    offset = nbr_ref[...] - own + REACH
    offset = jnp.where(offset < 0, offset + total, offset)
    offset = jnp.where(offset >= total, offset - total, offset)
    offset = jnp.where(rank < cnt_ref[...], offset, -1)
    for o in range(2 * REACH + 1):
        mult[o : o + 1, :] = jnp.sum(
            jnp.where(offset == o, 1.0, 0.0), axis=0, keepdims=True
        )
    mult[2 * REACH + 1 :, :] = jnp.zeros((mult.shape[0] - 2 * REACH - 1, rows), F32)

    z_1, z_2, z_3 = (zat(jnp.int32(k)) for k in (1, 2, 3))
    relay(jnp.int32(1), z_1)
    relay(jnp.int32(2), z_2)
    x_stage(blk, send_x1, send_c1, recv_1, core_1, 0, zi)
    for n in range(1, nx):
        staged(n - 1)
        coefficients(0, 0, n, zi * span + within[n], False)
    x_stage(blk, send_x1, send_c1, recv_1, core_1, 1, z_1)
    c_stage(blk, send_c1, core_1, 0, zi)
    for n in range(nx, span):
        staged(n - 1)
        coefficients(0, 0, n, zi * span + within[n], False)

    def first(g, zs):
        z_0, z_1 = zs
        z_2 = zat(g + 2)

        @pl.when(g + 2 < nz)
        def _():
            relay(g + 2, z_2)

        @pl.when(g + 1 < nz)
        def _():
            x_stage(blk, send_x1, send_c1, recv_1, core_1, g + 1, z_1)

        c_stage(blk, send_c1, core_1, g, z_0)

        @pl.when(g >= RING)
        def _():
            ring_write(g - RING).wait()

        slot = lax.rem(g, RING)
        for n in range(span):
            staged(n - 1)
            coefficients(g, slot, n, z_0 * span + within[n], False)
            if n == 0:
                ring_write(g - 1).start()
        return z_1, z_2

    lax.fori_loop(1, nz, first, (z_1, z_2))
    staged(span - 1)

    def sums():
        out = []
        for k in range(2):
            parts = acc[k]
            out.append((parts[0:32] + parts[32:64]) + parts[64:96])
        a, b = out
        row = lambda m, r: m[r : r + 1, :]
        bv = [row(b, 8 * c + 6) for c in range(3)]
        along = sum(xs[c] * bv[c] for c in range(3)) - row(b, 30)
        far = []
        for k in range(3):
            cross = sum(xs[c] * row(b, 8 * c + k) for c in range(3))
            far.append(
                FACT_A * row(a, 8 * k + 6)
                + FACT_B * ((xs[k] * along - cross) + row(b, 24 + k))
            )
        return far

    def place(b):
        return at(lax.div(b, span), lax.rem(lax.div(b, nc), nx), lax.rem(b, nc))

    before = place(lax.rem(order + tiles - 1, tiles))
    after = place(lax.rem(order + 1, tiles))

    def lubricated(rows_of):
        def six(s):
            return jnp.concatenate([blk[s][0:3, :], rows_of(s)], axis=0)

        wide = jnp.concatenate([six(before), six(me), six(after)], axis=1)
        mine = six(me)
        for o in range(2 * REACH + 1):
            begin = rows + o - REACH
            delta = mine - wide[:, begin : begin + rows]
            for k in range(6):
                lub[k, o : o + 1, :] = delta[k : k + 1, :]
        for k in range(6):
            lub[k, 2 * REACH + 1 :, :] = jnp.zeros((lub.shape[1] - 2 * REACH - 1, rows), F32)
        d = [lub[k] for k in range(3)]
        e = [lub[3 + k] for k in range(3)]
        square = d[0] * d[0] + d[1] * d[1] + d[2] * d[2] + SOFT
        dist = jnp.sqrt(square)
        strength = mult[...] / ((0.5 + jnp.abs(dist - 2.0)) * square)
        force = strength * (d[0] * e[0] + d[1] * e[1] + d[2] * e[2])
        return [jnp.sum(force * d[k], axis=0, keepdims=True) for k in range(3)]

    rhs = [rhs_ref[k : k + 1, :] for k in range(3)]
    far = sums()
    near_part = lubricated(lambda s: blk[s][3:6, :])
    work = [far[k] + near_part[k] for k in range(3)]
    inner = lambda u, v: total_of(u[0] * v[0] + u[1] * v[1] + u[2] * v[2])
    lane = lax.broadcasted_iota(jnp.int32, (1, rows), 1)

    def packed(values):
        line = jnp.zeros((1, rows), F32)
        for k, value in enumerate(values):
            line = jnp.where(lane == k, value, line)
        return line

    def unpacked(line, count):
        return [
            jnp.sum(jnp.where(lane[:, : line.shape[1]] == k, line, 0.0), axis=1, keepdims=True)
            for k in range(count)
        ]

    vec[me] = jnp.concatenate(
        work + [packed([inner(rhs, rhs), inner(work, rhs), inner(work, work)])], axis=0
    )

    def z_copy(k):
        return copy(vec, me, send_z2.at[k], recv_2.at[me], {"blk_0": zat(k)})

    def z_start(k, _):
        z_copy(k).start()
        return 0

    for c in x_copies(vec, me, send_x2, recv_2, 0):
        c.start()
    lax.fori_loop(1, nz, z_start, 0)

    def last_writes(g, _):
        ring_write(g).wait()
        return 0

    ring_write(jnp.int32(nz - 1)).start()
    lax.fori_loop(max(nz - RING, 0), nz, last_writes, 0)
    for g in range(min(RING, nz)):
        ring_read(jnp.int32(g)).start()
    acc[...] = jnp.zeros(acc.shape, F32)
    tot[...] = jnp.zeros(tot.shape, F32)

    def z_second(g):
        z_stage(vec, send_x2, recv_2, g, zat(g))

    def x_second(g):
        x_stage(vec, send_x2, send_c2, recv_2, core_2, g, zat(g))

    def second(g, _):
        @pl.when(g + LOOK_Z < nz)
        def _():
            z_second(g + LOOK_Z)

        @pl.when(g + LOOK_X < nz)
        def _():
            x_second(g + LOOK_X)

        z_0 = zat(g)
        c_stage(vec, send_c2, core_2, g, z_0)
        ring_read(g).wait()
        slot = lax.rem(g, RING)
        sum_a = sum_b = None
        sum_v = tot[...]
        for n in range(span):
            s = z_0 * span + within[n]
            v = vec[s]
            sum_v = sum_v + v
            weights(centred(s), [v[c : c + 1, :] for c in range(3)], wsts[n % 2])
            w = wsts[n % 2][...]
            for k in range(2):
                part = dot(w, ring[slot, 2 * n + k])
                sum_a = part if sum_a is None else sum_a + part
            for k in range(3):
                part = dot(w, keep_b[g * span + n, k])
                sum_b = part if sum_b is None else sum_b + part
        tot[...] = sum_v
        acc[0] += sum_a
        acc[1] += sum_b

        @pl.when(g + RING < nz)
        def _():
            ring_read(g + RING).start()

        return 0

    z_second(jnp.int32(1))
    z_second(jnp.int32(2))
    x_second(jnp.int32(0))
    for g in range(3, min(LOOK_Z, nz)):
        z_second(jnp.int32(g))
    for g in range(1, min(LOOK_X, nz)):
        x_second(jnp.int32(g))
    lax.fori_loop(0, nz, second, 0)

    far = sums()
    near_part = lubricated(lambda s: vec[s][0:3, :])
    again = [far[k] + near_part[k] for k in range(3)]

    rr, wr, ww = unpacked(tot[3:4, :], 3)
    beta = jnp.sqrt(rr + EPS)
    image_0 = [work[k] / beta for k in range(3)]
    v_0 = [rhs[k] / beta for k in range(3)]
    h_00 = wr / (beta * beta)
    h_10 = jnp.sqrt(ww / (beta * beta) - h_00 * h_00 + EPS)
    v_1 = [(image_0[k] - h_00 * v_0[k]) / h_10 for k in range(3)]
    image_1 = [(again[k] / beta - h_00 * image_0[k]) / h_10 for k in range(3)]
    line = packed([inner(image_1, v_0), inner(image_1, v_1), inner(image_1, image_1)])[:, :128]

    base = 0
    for buf, mine, count, name in (
        (red_c, ci, nc, "blk_2"), (red_x, xi, nx, "blk_1"), (red_z, zi, nz, "blk_0")
    ):
        others = [lax.rem(mine + k, count) for k in range(1, count)]
        buf[mine] = line
        copies = [
            copy(buf, mine, send_3.at[base + k], recv_3.at[base + mine], {name: other})
            for k, other in enumerate(others)
        ]
        for c in copies:
            c.start()
        for k, other in enumerate(others):
            copy(buf, other, send_3.at[base + k], recv_3.at[base + other], up).wait_recv()
        line = buf[0]
        for k in range(1, count):
            line = line + buf[k]
        for c in copies:
            c.wait_send()
        base += count
    h_01, h_11, squares = unpacked(line, 3)
    h_21 = jnp.sqrt(squares - h_01 * h_01 - h_11 * h_11 + EPS)

    rho_0 = jnp.sqrt(h_00 * h_00 + h_10 * h_10)
    c_0, s_0 = h_00 / rho_0, h_10 / rho_0
    g_1 = -s_0 * beta
    g_0 = c_0 * beta
    r_01 = c_0 * h_01 + s_0 * h_11
    r_11 = c_0 * h_11 - s_0 * h_01
    rho_1 = jnp.sqrt(r_11 * r_11 + h_21 * h_21)
    g_1 = (r_11 / rho_1) * g_1
    y_1 = g_1 / rho_1
    y_0 = (g_0 - r_01 * y_1) / rho_0
    for k in range(3):
        out_ref[0, k : k + 1, :] = y_0 * v_0[k] + y_1 * v_1[k]
        out_ref[1, k : k + 1, :] = rhs[k] - y_0 * image_0[k] - y_1 * image_1[k]

    def z_done(k, _):
        z_copy(k).wait_send()
        return 0

    lax.fori_loop(1, nz, z_done, 0)

    def relay_done(g, _):
        copy(blk, me, send_z1.at[g], recv_1.at[me], up).wait_send()
        return 0

    lax.fori_loop(0, nz - 1, relay_done, 0)
    finish_sends(blk, send_x1, send_c1, recv_1, core_1)
    finish_sends(vec, send_x2, send_c2, recv_2, core_2)


def on_device(positions, right_side, neighbours, counts):
    rows = positions.shape[1]
    sizes = nz, nx, nc = tuple(lax.axis_size(a) for a in AXES)
    span = nx * nc
    tiles = nz * span
    slots = 8 * -(-(2 * REACH + 1) // 8)
    vmem = pl.BlockSpec(memory_space=pltpu.VMEM)
    dma = pltpu.SemaphoreType.DMA
    gather_sems = [dma((tiles,)), dma((nz,)), dma((nz + 1,)), dma((nz, nx - 1)), dma((nz,))]
    out, _ = pl.pallas_call(
        functools.partial(kernel, sizes, rows),
        out_shape=(
            jax.ShapeDtypeStruct((2, 3, rows), F32),
            jax.ShapeDtypeStruct((nz, 2 * span, rows, rows), BF16),
        ),
        in_specs=[vmem] * 4,
        out_specs=(vmem, pl.BlockSpec(memory_space=pltpu.HBM)),
        scratch_shapes=[
            pltpu.VMEM((tiles, 8, rows), F32),
            pltpu.VMEM((tiles, 4, rows), F32),
            pltpu.VMEM((nc, 1, 128), F32),
            pltpu.VMEM((nx, 1, 128), F32),
            pltpu.VMEM((nz, 1, 128), F32),
            pltpu.VMEM((tiles, 3, rows, rows), BF16),
            pltpu.VMEM((RING, 2 * span, rows, rows), BF16),
            pltpu.VMEM((5, rows, rows), BF16),
            pltpu.VMEM((5, rows, rows), BF16),
            pltpu.VMEM((96, rows), BF16),
            pltpu.VMEM((96, rows), BF16),
            pltpu.VMEM((2, 96, rows), F32),
            pltpu.VMEM((slots, rows), F32),
            pltpu.VMEM((8, rows), F32),
            pltpu.VMEM((8, rows), F32),
            pltpu.VMEM((6, slots, rows), F32),
            pltpu.VMEM((4, rows), F32),
        ]
        + gather_sems * 2
        + [dma((nz + nx + nc,)), dma((nz + nx + nc,)), dma((RING,)), dma((RING,))],
        compiler_params=pltpu.CompilerParams(
            collective_id=0, has_side_effects=True, vmem_limit_bytes=67043328
        ),
    )(positions, right_side, neighbours, counts[None, :])
    return out[0], out[1]


def solution(mesh):
    torus = Mesh(mesh.devices.reshape(mesh.shape["groups"], 16, 4, 2), GROUPS_BLK)
    placed = (P(None, GROUPS_BLK), P(None, GROUPS_BLK), P(None, GROUPS_BLK), P(GROUPS_BLK))
    return jax.shard_map(
        on_device,
        mesh=torus,
        in_specs=placed,
        out_specs=(P(None, GROUPS_BLK), P(None, GROUPS_BLK)),
        check_vma=False,
    )
```

time: 157 us -> 122 us (0.78)
  Pallas kernels: 154 us -> 120 us
    pallas_call x1, Pallas kernels: 154 us -> 120 us  [on_device(): pl.pallas_call(functools.partial(kernel, sizes, rows), out_shape=(jax.Sha...]
    unnamed x2 -> x0, local copies, waits for them, and re-layouts: 2.55 us -> none
where the time goes in v2:
time: 122 us
  Pallas kernels  120 us (98%)
  local copies, waits for them, and re-layouts  1.28 us (1%)
    pallas_call x1, Pallas kernels, on_device(): pl.pallas_call(functools.partial(kernel, sizes, rows), out_shape=(jax.Sha...  120 us

profile of v2, /device:TPU:40, one launch (start us, length us, event | category | flops | bytes accessed | tf_op | source)
XLA Modules:
  0.0 121.8 jit_solution(6424814406988261726)
XLA Ops:
  0.6 119.9 %shard_map.59 = (f32[2,3,256]{2,1,0:T(4,128)}, bf16[16,16,256,256]{3,2,1,0:T(8,128)(2,1)}) custom-call(f32[3,256]{1,0:T(4,128)} %pos_ref.1, f32[3,256]{1,0:T(4,128)} %rhs_ref.1, s32[16,256]{1,0:T(8,128)} %nbr_ref.1, s32[1,256]{1,0:T(1,128)} %bitcast.5), custom_call_target="tpu_custom_call" | custom-call | tf_op jit(solution)/shard_map/pallas_call | solution.py:485
  120.5 1.3 %slice_bitcast_fusion = (f32[3,256]{1,0:T(4,128)}, f32[3,256]{1,0:T(4,128)}) fusion(f32[2,3,256]{2,1,0:T(4,128)} %get-tuple-element.3), kind=kLoop, calls=%fused_computation | loop fusion | bytes 12288 | tf_op jit(solution)/shard_map/squeeze | solution.py:518

commit v3 on v2

--- a/solution.py
+++ b/solution.py
@@ -24,7 +24,7 @@
 
 RING = 4
 CHUNK = 32
-LOOK_Z, LOOK_X = 6, 2
+LOOK_Z, LOOK_X = 4, 1
 
 
 def hop(k):
@@ -51,9 +51,9 @@
     out_ref, a_hbm,
     blk, vec, red_c, red_x, red_z,
     keep_b, ring, stage_0, stage_1, wst_0, wst_1, acc, mult, centre, scale, lub, tot,
-    recv_1, core_1, send_z1, send_x1, send_c1,
-    recv_2, core_2, send_z2, send_x2, send_c2,
-    recv_3, send_3, ring_out, ring_in,
+    spread,
+    from_z1, from_x1, core_1, send_1, from_z2, from_x2, core_2, send_2, from_3, send_3,
+    ring_out, ring_in,
 ):
     nz, nx, nc = sizes
     span = nx * nc
@@ -101,53 +101,45 @@
     down = {"blk_0": lax.rem(zi + nz - 1, nz)}
     beside = {"blk_2": cat[nc - 1]}
 
-    def x_copies(buf, s, send, recv, g):
-        return [
-            copy(buf, s, send.at[g, k - 1], recv.at[s], {"blk_1": xat[k]}) for k in range(1, nx)
-        ]
-
-    def c_copy(buf, send, core, g, z, c):
-        return copy(buf, pl.ds((z * nc + c) * nx, nx), send.at[g], core.at[z], beside)
-
-    def z_stage(buf, send_x, recv, g, z):
+    def x_copies(buf, s, send, recv, z):
+        return [copy(buf, s, send.at[1], recv.at[z], {"blk_1": x}) for x in xat[1:]]
+
+    def c_copy(buf, send, core, z, c):
+        return copy(buf, pl.ds((z * nc + c) * nx, nx), send.at[2], core.at[z], beside)
+
+    def z_stage(buf, send, from_z, from_x, z):
         s = at(z, xi, ci)
-        copy(buf, s, send_x.at[g, 0], recv.at[s], up).wait_recv()
-        for c in x_copies(buf, s, send_x, recv, g):
+        copy(buf, s, send.at[0], from_z.at[z], up).wait_recv()
+        for c in x_copies(buf, s, send, from_x, z):
             c.start()
 
-    def x_stage(buf, send_x, send_c, recv, core, g, z):
-        for k in range(1, nx):
-            s = at(z, xat[k], ci)
-            copy(buf, s, send_x.at[g, 0], recv.at[s], up).wait_recv()
-        c_copy(buf, send_c, core, g, z, ci).start()
-
-    def c_stage(buf, send_c, core, g, z):
-        c_copy(buf, send_c, core, g, z, cat[nc - 1]).wait_recv()
+    def x_stage(buf, send, from_x, core, z):
+        some = pl.ds((z * nc + ci) * nx, nx - 1)
+        copy(buf, some, send.at[1], from_x.at[z], up).wait_recv()
+        c_copy(buf, send, core, z, ci).start()
+
+    def c_stage(buf, send, core, z):
+        c_copy(buf, send, core, z, cat[nc - 1]).wait_recv()
 
     def relay(g, z):
         s = at(z, xi, ci)
-        copy(blk, s, send_z1.at[0], recv_1.at[s], up).wait_recv()
+        copy(blk, s, send_1.at[0], from_z1.at[z], up).wait_recv()
         j, odd = lax.div(g + 1, 2), lax.rem(g, 2)
 
         @pl.when((odd == 1) & (j < plus))
         def _():
-            copy(blk, s, send_z1.at[g + 1], recv_1.at[s], down).start()
+            copy(blk, s, send_1.at[0], from_z1.at[z], down).start()
 
         @pl.when((odd == 0) & (j < nz - 1 - plus))
         def _():
-            copy(blk, s, send_z1.at[g + 1], recv_1.at[s], up).start()
-
-        for c in x_copies(blk, s, send_x1, recv_1, g):
+            copy(blk, s, send_1.at[0], from_z1.at[z], up).start()
+
+        for c in x_copies(blk, s, send_1, from_x1, z):
             c.start()
 
-    def finish_sends(buf, send_x, send_c, recv, core):
-        def body(g, _):
-            for c in x_copies(buf, me, send_x, recv, g):
-                c.wait_send()
-            c_copy(buf, send_c, core, g, g, ci).wait_send()
-            return 0
-
-        lax.fori_loop(0, nz, body, 0)
+    def finish_sends(buf, send, from_z):
+        for kind, count in enumerate((nz - 1, nz * (nx - 1), nz * nx)):
+            copy(buf, pl.ds(0, count), send.at[kind], from_z.at[0], up).wait_send()
 
     own_row = (blk[me] - centre[...]) * scale[...]
     xs = [own_row[c : c + 1, :] for c in range(3)]
@@ -163,15 +155,37 @@
         for k, part in enumerate(limbs(jnp.concatenate(columns, axis=0), 3)):
             out[32 * k : 32 * (k + 1), :] = part
 
-    def coefficients(g, slot, n, s, masked):
-        stage, t = stages[n % 2], g * span + n
+    def prepare(s, n):
         block = centred(s)
         raw = blk[s]
         weights(block, [raw[3 + c : 4 + c, :] for c in range(3)], wsts[n % 2])
-        turned = block.T
+        return block.T
+
+    def prepare_ahead(s, n):
+        turned = prepare(s, n)
+        for c in range(3):
+            spread[c] = jnp.broadcast_to(turned[:, c : c + 1], (rows, 128))
+
+    def coefficients(g, slot, n, s, masked=False, ahead=False):
+        stage, t = stages[n % 2], g * span + n
+        turned = None if ahead else prepare(s, n)
+
+        def put(x, k, part, keep):
+            stage[k, part, :] = x.astype(BF16)
+            piece = stage[k, part, :]
+            keep[part, :] = piece
+            return x - piece.astype(F32)
+
         for j in range(rows // CHUNK):
             part = slice(j * CHUNK, (j + 1) * CHUNK)
-            dx, dy, dz = (turned[part, c : c + 1] - xs[c] for c in range(3))
+            if ahead:
+                ds = [
+                    jnp.concatenate([spread[c, part, :]] * (rows // 128), axis=1) - xs[c]
+                    for c in range(3)
+                ]
+            else:
+                ds = [turned[part, c : c + 1] - xs[c] for c in range(3)]
+            dx, dy, dz = ds
             square = (dx * dx + dy * dy) + (dz * dz + SOFT * 0.75)
             q = lax.rsqrt(square)
             q_far = jnp.minimum(q, 1.0 / EDGE)
@@ -182,12 +196,10 @@
                 first = lax.broadcasted_iota(jnp.int32, b.shape, 0) + j * CHUNK
                 second = lax.broadcasted_iota(jnp.int32, b.shape, 1)
                 b = jnp.where(first == second, 0.0, b)
-            for k, piece in enumerate(limbs(a, 2)):
-                stage[k, part, :] = piece
-                ring[slot, 2 * n + k, part, :] = piece
-            for k, piece in enumerate(limbs(b, 3)):
-                stage[2 + k, part, :] = piece
-                keep_b[t, k, part, :] = piece
+            for k in range(2):
+                a = put(a, k, part, ring.at[slot, 2 * n + k])
+            for k in range(3):
+                b = put(b, 2 + k, part, keep_b.at[t, k])
 
     def dot(w, m):
         return jnp.dot(w, m, preferred_element_type=F32)
@@ -205,11 +217,11 @@
         slot = lax.rem(g, RING)
         return pltpu.make_async_copy(a_hbm.at[g], ring.at[slot], ring_in.at[slot])
 
-    copy(blk, me, send_z1.at[0], recv_1.at[me], up).start()
-    copy(blk, me, send_z1.at[1], recv_1.at[me], down).start()
-    for c in x_copies(blk, me, send_x1, recv_1, 0):
+    copy(blk, me, send_1.at[0], from_z1.at[zi], up).start()
+    copy(blk, me, send_1.at[0], from_z1.at[zi], down).start()
+    for c in x_copies(blk, me, send_1, from_x1, zi):
         c.start()
-    coefficients(0, 0, 0, me, True)
+    coefficients(0, 0, 0, me, masked=True)
 
     own = order * rows + lax.broadcasted_iota(jnp.int32, nbr_ref.shape, 1)
     rank = lax.broadcasted_iota(jnp.int32, nbr_ref.shape, 0)
@@ -223,18 +235,19 @@
         )
     mult[2 * REACH + 1 :, :] = jnp.zeros((mult.shape[0] - 2 * REACH - 1, rows), F32)
 
-    z_1, z_2, z_3 = (zat(jnp.int32(k)) for k in (1, 2, 3))
+    z_1, z_2 = (zat(jnp.int32(k)) for k in (1, 2))
     relay(jnp.int32(1), z_1)
     relay(jnp.int32(2), z_2)
-    x_stage(blk, send_x1, send_c1, recv_1, core_1, 0, zi)
+    x_stage(blk, send_1, from_x1, core_1, zi)
     for n in range(1, nx):
         staged(n - 1)
-        coefficients(0, 0, n, zi * span + within[n], False)
-    x_stage(blk, send_x1, send_c1, recv_1, core_1, 1, z_1)
-    c_stage(blk, send_c1, core_1, 0, zi)
+        coefficients(0, 0, n, zi * span + within[n])
+    c_stage(blk, send_1, core_1, zi)
     for n in range(nx, span):
         staged(n - 1)
-        coefficients(0, 0, n, zi * span + within[n], False)
+        coefficients(0, 0, n, zi * span + within[n])
+    prepare_ahead(z_1 * span + within[0], 0)
+    x_stage(blk, send_1, from_x1, core_1, z_1)
 
     def first(g, zs):
         z_0, z_1 = zs
@@ -246,9 +259,9 @@
 
         @pl.when(g + 1 < nz)
         def _():
-            x_stage(blk, send_x1, send_c1, recv_1, core_1, g + 1, z_1)
-
-        c_stage(blk, send_c1, core_1, g, z_0)
+            x_stage(blk, send_1, from_x1, core_1, z_1)
+
+        c_stage(blk, send_1, core_1, z_0)
 
         @pl.when(g >= RING)
         def _():
@@ -257,9 +270,10 @@
         slot = lax.rem(g, RING)
         for n in range(span):
             staged(n - 1)
-            coefficients(g, slot, n, z_0 * span + within[n], False)
+            coefficients(g, slot, n, z_0 * span + within[n], ahead=n == 0)
             if n == 0:
                 ring_write(g - 1).start()
+        prepare_ahead(z_1 * span + within[0], 0)
         return z_1, z_2
 
     lax.fori_loop(1, nz, first, (z_1, z_2))
@@ -334,13 +348,13 @@
     )
 
     def z_copy(k):
-        return copy(vec, me, send_z2.at[k], recv_2.at[me], {"blk_0": zat(k)})
+        return copy(vec, me, send_2.at[0], from_z2.at[zi], {"blk_0": zat(k)})
 
     def z_start(k, _):
         z_copy(k).start()
         return 0
 
-    for c in x_copies(vec, me, send_x2, recv_2, 0):
+    for c in x_copies(vec, me, send_2, from_x2, zi):
         c.start()
     lax.fori_loop(1, nz, z_start, 0)
 
@@ -349,17 +363,14 @@
         return 0
 
     ring_write(jnp.int32(nz - 1)).start()
-    lax.fori_loop(max(nz - RING, 0), nz, last_writes, 0)
-    for g in range(min(RING, nz)):
-        ring_read(jnp.int32(g)).start()
     acc[...] = jnp.zeros(acc.shape, F32)
     tot[...] = jnp.zeros(tot.shape, F32)
 
     def z_second(g):
-        z_stage(vec, send_x2, recv_2, g, zat(g))
+        z_stage(vec, send_2, from_z2, from_x2, zat(g))
 
     def x_second(g):
-        x_stage(vec, send_x2, send_c2, recv_2, core_2, g, zat(g))
+        x_stage(vec, send_2, from_x2, core_2, zat(g))
 
     def second(g, _):
         @pl.when(g + LOOK_Z < nz)
@@ -371,7 +382,7 @@
             x_second(g + LOOK_X)
 
         z_0 = zat(g)
-        c_stage(vec, send_c2, core_2, g, z_0)
+        c_stage(vec, send_2, core_2, z_0)
         ring_read(g).wait()
         slot = lax.rem(g, RING)
         sum_a = sum_b = None
@@ -398,13 +409,15 @@
 
         return 0
 
-    z_second(jnp.int32(1))
-    z_second(jnp.int32(2))
-    x_second(jnp.int32(0))
+    for g in range(1, min(3, LOOK_Z, nz)):
+        z_second(jnp.int32(g))
+    lax.fori_loop(max(nz - RING, 0), nz, last_writes, 0)
+    for g in range(min(RING, nz)):
+        ring_read(jnp.int32(g)).start()
+    for g in range(0, min(LOOK_X, nz)):
+        x_second(jnp.int32(g))
     for g in range(3, min(LOOK_Z, nz)):
         z_second(jnp.int32(g))
-    for g in range(1, min(LOOK_X, nz)):
-        x_second(jnp.int32(g))
     lax.fori_loop(0, nz, second, 0)
 
     far = sums()
@@ -421,26 +434,22 @@
     image_1 = [(again[k] / beta - h_00 * image_0[k]) / h_10 for k in range(3)]
     line = packed([inner(image_1, v_0), inner(image_1, v_1), inner(image_1, image_1)])[:, :128]
 
-    base = 0
-    for buf, mine, count, name in (
-        (red_c, ci, nc, "blk_2"), (red_x, xi, nx, "blk_1"), (red_z, zi, nz, "blk_0")
+    for level, (buf, mine, count, name) in enumerate(
+        ((red_c, ci, nc, "blk_2"), (red_x, xi, nx, "blk_1"), (red_z, zi, nz, "blk_0"))
     ):
         others = [lax.rem(mine + k, count) for k in range(1, count)]
         buf[mine] = line
         copies = [
-            copy(buf, mine, send_3.at[base + k], recv_3.at[base + mine], {name: other})
-            for k, other in enumerate(others)
+            copy(buf, mine, send_3.at[level], from_3.at[level], {name: other}) for other in others
         ]
         for c in copies:
             c.start()
-        for k, other in enumerate(others):
-            copy(buf, other, send_3.at[base + k], recv_3.at[base + other], up).wait_recv()
+        everyone = copy(buf, pl.ds(0, count - 1), send_3.at[level], from_3.at[level], up)
+        everyone.wait_recv()
         line = buf[0]
         for k in range(1, count):
             line = line + buf[k]
-        for c in copies:
-            c.wait_send()
-        base += count
+        everyone.wait_send()
     h_01, h_11, squares = unpacked(line, 3)
     h_21 = jnp.sqrt(squares - h_01 * h_01 - h_11 * h_11 + EPS)
 
@@ -458,19 +467,8 @@
         out_ref[0, k : k + 1, :] = y_0 * v_0[k] + y_1 * v_1[k]
         out_ref[1, k : k + 1, :] = rhs[k] - y_0 * image_0[k] - y_1 * image_1[k]
 
-    def z_done(k, _):
-        z_copy(k).wait_send()
-        return 0
-
-    lax.fori_loop(1, nz, z_done, 0)
-
-    def relay_done(g, _):
-        copy(blk, me, send_z1.at[g], recv_1.at[me], up).wait_send()
-        return 0
-
-    lax.fori_loop(0, nz - 1, relay_done, 0)
-    finish_sends(blk, send_x1, send_c1, recv_1, core_1)
-    finish_sends(vec, send_x2, send_c2, recv_2, core_2)
+    finish_sends(blk, send_1, from_z1)
+    finish_sends(vec, send_2, from_z2)
 
 
 def on_device(positions, right_side, neighbours, counts):
@@ -481,7 +479,7 @@
     slots = 8 * -(-(2 * REACH + 1) // 8)
     vmem = pl.BlockSpec(memory_space=pltpu.VMEM)
     dma = pltpu.SemaphoreType.DMA
-    gather_sems = [dma((tiles,)), dma((nz,)), dma((nz + 1,)), dma((nz, nx - 1)), dma((nz,))]
+    gather_sems = [dma((nz,)), dma((nz,)), dma((nz,)), dma((3,))]
     out, _ = pl.pallas_call(
         functools.partial(kernel, sizes, rows),
         out_shape=(
@@ -508,9 +506,10 @@
             pltpu.VMEM((8, rows), F32),
             pltpu.VMEM((6, slots, rows), F32),
             pltpu.VMEM((4, rows), F32),
+            pltpu.VMEM((3, rows, 128), F32),
         ]
         + gather_sems * 2
-        + [dma((nz + nx + nc,)), dma((nz + nx + nc,)), dma((RING,)), dma((RING,))],
+        + [dma((3,)), dma((3,)), dma((RING,)), dma((RING,))],
         compiler_params=pltpu.CompilerParams(
             collective_id=0, has_side_effects=True, vmem_limit_bytes=67043328
         ),

time: 122 us -> 115 us (0.943)
  Pallas kernels: 120 us -> 113 us
    pallas_call x1, Pallas kernels: 120 us -> 113 us  [on_device(): pl.pallas_call(functools.partial(kernel, sizes, rows), out_shape=(jax.Sha...]
where the time goes in v3:
time: 115 us
  Pallas kernels  113 us (98%)
  local copies, waits for them, and re-layouts  1.28 us (1%)
    pallas_call x1, Pallas kernels, on_device(): pl.pallas_call(functools.partial(kernel, sizes, rows), out_shape=(jax.Sha...  113 us

profile of v3, /device:TPU:40, one launch (start us, length us, event | category | flops | bytes accessed | tf_op | source)
XLA Modules:
  0.0 115.2 jit_solution(17985917053989619684)
XLA Ops:
  0.6 113.3 %shard_map.59 = (f32[2,3,256]{2,1,0:T(4,128)}, bf16[16,16,256,256]{3,2,1,0:T(8,128)(2,1)}) custom-call(f32[3,256]{1,0:T(4,128)} %pos_ref.1, f32[3,256]{1,0:T(4,128)} %rhs_ref.1, s32[16,256]{1,0:T(8,128)} %nbr_ref.1, s32[1,256]{1,0:T(1,128)} %bitcast.5), custom_call_target="tpu_custom_call" | custom-call | tf_op jit(solution)/shard_map/pallas_call | solution.py:483
  113.9 1.3 %slice_bitcast_fusion = (f32[3,256]{1,0:T(4,128)}, f32[3,256]{1,0:T(4,128)}) fusion(f32[2,3,256]{2,1,0:T(4,128)} %get-tuple-element.3), kind=kLoop, calls=%fused_computation | loop fusion | bytes 12288 | tf_op jit(solution)/shard_map/squeeze | solution.py:517

commit v4 on v3

--- a/solution.py
+++ b/solution.py
@@ -13,18 +13,20 @@
 AXES = ("blk_0", "blk_1", "blk_2")
 GROUPS_BLK = ("groups",) + AXES
 MESH = pl.DeviceIdType.MESH
-F32, BF16 = jnp.float32, jnp.bfloat16
+F32, BF16, F8 = jnp.float32, jnp.bfloat16, jnp.float8_e4m3fn
 
 SOFT = 0.0001
 EPS = 1e-06
+K = 24.0
 G = math.sqrt(0.75)
-EDGE = 2.0 * G
-FACT_A = 0.375 * G
-FACT_B = 1.125 * G
-
-RING = 4
+SCALE = G / K
+EDGE = 2.0 * SCALE
+FACT_A = 0.375 * G / K**3
+FACT_B = 1.125 * G / K**3
+
+RING = 3
 CHUNK = 32
-LOOK_Z, LOOK_X = 4, 1
+LOOK_Z, LOOK_X = 7, 2
 
 
 def hop(k):
@@ -50,7 +52,7 @@
     pos_ref, rhs_ref, nbr_ref, cnt_ref,
     out_ref, a_hbm,
     blk, vec, red_c, red_x, red_z,
-    keep_b, ring, stage_0, stage_1, wst_0, wst_1, acc, mult, centre, scale, lub, tot,
+    keep, keep_8, ring, stage_0, stage_1, stage_80, stage_81, wst_0, wst_1, acc, mult, centre, scale, lub, tot,
     spread,
     from_z1, from_x1, core_1, send_1, from_z2, from_x2, core_2, send_2, from_3, send_3,
     ring_out, ring_in,
@@ -68,7 +70,7 @@
     me = at(zi, xi, ci)
     within = [cat[d] * nx + xat[k] for d in range(nc) for k in range(nx)]
     plus = nz // 2
-    stages, wsts = (stage_0, stage_1), (wst_0, wst_1)
+    stages, stages_8, wsts = (stage_0, stage_1), (stage_80, stage_81), (wst_0, wst_1)
 
     barrier = pltpu.get_barrier_semaphore()
     near = []
@@ -87,7 +89,7 @@
         [jnp.broadcast_to(middle, (3, rows)), jnp.zeros((5, rows), F32)], axis=0
     )
     line = lax.broadcasted_iota(jnp.int32, (8, rows), 0)
-    scale[...] = jnp.where(line < 3, G, 1.0).astype(F32)
+    scale[...] = jnp.where(line < 3, SCALE, 1.0).astype(F32)
     acc[...] = jnp.zeros(acc.shape, F32)
     pl.semaphore_wait(barrier, len(near))
 
@@ -167,14 +169,18 @@
             spread[c] = jnp.broadcast_to(turned[:, c : c + 1], (rows, 128))
 
     def coefficients(g, slot, n, s, masked=False, ahead=False):
-        stage, t = stages[n % 2], g * span + n
+        stage, stage_8, t = stages[n % 2], stages_8[n % 2], g * span + n
         turned = None if ahead else prepare(s, n)
 
-        def put(x, k, part, keep):
+        def put(x, k, part):
             stage[k, part, :] = x.astype(BF16)
             piece = stage[k, part, :]
-            keep[part, :] = piece
+            keep[t, k, part, :] = piece
             return x - piece.astype(F32)
+
+        def put_last(x, k, part, kept):
+            stage_8[k, part, :] = x.astype(F8)
+            kept[part, :] = stage_8[k, part, :]
 
         for j in range(rows // CHUNK):
             part = slice(j * CHUNK, (j + 1) * CHUNK)
@@ -186,28 +192,27 @@
             else:
                 ds = [turned[part, c : c + 1] - xs[c] for c in range(3)]
             dx, dy, dz = ds
-            square = (dx * dx + dy * dy) + (dz * dz + SOFT * 0.75)
+            square = (dx * dx + dy * dy) + (dz * dz + SOFT * SCALE * SCALE)
             q = lax.rsqrt(square)
             q_far = jnp.minimum(q, 1.0 / EDGE)
             q2 = q_far * q_far
-            a = q_far * (q2 + 2.0) + jnp.maximum(EDGE - square * q, 0.0)
-            b = (q * q2) * (2.0 / 3.0 - q2)
+            close = jnp.maximum(EDGE * K**4 - square * (q * K**4), 0.0)
+            a = q_far * (q2 + 2.0 * K * K) + close
+            b = (q * q2) * (2.0 / 3.0 * K * K - q2)
             if masked:
                 first = lax.broadcasted_iota(jnp.int32, b.shape, 0) + j * CHUNK
                 second = lax.broadcasted_iota(jnp.int32, b.shape, 1)
                 b = jnp.where(first == second, 0.0, b)
-            for k in range(2):
-                a = put(a, k, part, ring.at[slot, 2 * n + k])
-            for k in range(3):
-                b = put(b, 2 + k, part, keep_b.at[t, k])
+            put_last(put(a, 0, part), 0, part, ring.at[slot, n])
+            put_last(put(put(b, 1, part), 2, part), 1, part, keep_8.at[t])
 
     def dot(w, m):
         return jnp.dot(w, m, preferred_element_type=F32)
 
     def staged(n):
-        stage, w = stages[n % 2], wsts[n % 2][...]
-        acc[0] += dot(w, stage[0]) + dot(w, stage[1])
-        acc[1] += dot(w, stage[2]) + dot(w, stage[3]) + dot(w, stage[4])
+        stage, stage_8, w = stages[n % 2], stages_8[n % 2], wsts[n % 2][...]
+        acc[0] += dot(w, stage[0]) + dot(w, stage_8[0])
+        acc[1] += dot(w, stage[1]) + dot(w, stage[2]) + dot(w, stage_8[1])
 
     def ring_write(g):
         slot = lax.rem(g, RING)
@@ -248,14 +253,16 @@
         coefficients(0, 0, n, zi * span + within[n])
     prepare_ahead(z_1 * span + within[0], 0)
     x_stage(blk, send_1, from_x1, core_1, z_1)
+    z_3 = zat(jnp.int32(3))
+    relay(jnp.int32(3), z_3)
 
     def first(g, zs):
-        z_0, z_1 = zs
-        z_2 = zat(g + 2)
-
-        @pl.when(g + 2 < nz)
-        def _():
-            relay(g + 2, z_2)
+        z_0, z_1, z_2 = zs
+        z_3 = zat(g + 3)
+
+        @pl.when(g + 3 < nz)
+        def _():
+            relay(g + 3, z_3)
 
         @pl.when(g + 1 < nz)
         def _():
@@ -267,16 +274,15 @@
         def _():
             ring_write(g - RING).wait()
 
+        ring_write(g - 1).start()
         slot = lax.rem(g, RING)
         for n in range(span):
             staged(n - 1)
             coefficients(g, slot, n, z_0 * span + within[n], ahead=n == 0)
-            if n == 0:
-                ring_write(g - 1).start()
         prepare_ahead(z_1 * span + within[0], 0)
-        return z_1, z_2
-
-    lax.fori_loop(1, nz, first, (z_1, z_2))
+        return z_1, z_2, z_3
+
+    lax.fori_loop(1, nz, first, (z_1, z_2, z_3))
     staged(span - 1)
 
     def sums():
@@ -393,12 +399,11 @@
             sum_v = sum_v + v
             weights(centred(s), [v[c : c + 1, :] for c in range(3)], wsts[n % 2])
             w = wsts[n % 2][...]
-            for k in range(2):
-                part = dot(w, ring[slot, 2 * n + k])
-                sum_a = part if sum_a is None else sum_a + part
-            for k in range(3):
-                part = dot(w, keep_b[g * span + n, k])
-                sum_b = part if sum_b is None else sum_b + part
+            t = g * span + n
+            part = dot(w, keep[t, 0]) + dot(w, ring[slot, n])
+            sum_a = part if sum_a is None else sum_a + part
+            part = dot(w, keep[t, 1]) + dot(w, keep[t, 2]) + dot(w, keep_8[t])
+            sum_b = part if sum_b is None else sum_b + part
         tot[...] = sum_v
         acc[0] += sum_a
         acc[1] += sum_b
@@ -414,10 +419,11 @@
     lax.fori_loop(max(nz - RING, 0), nz, last_writes, 0)
     for g in range(min(RING, nz)):
         ring_read(jnp.int32(g)).start()
-    for g in range(0, min(LOOK_X, nz)):
-        x_second(jnp.int32(g))
+    x_second(jnp.int32(0))
     for g in range(3, min(LOOK_Z, nz)):
         z_second(jnp.int32(g))
+    for g in range(1, min(LOOK_X, nz)):
+        x_second(jnp.int32(g))
     lax.fori_loop(0, nz, second, 0)
 
     far = sums()
@@ -484,7 +490,7 @@
         functools.partial(kernel, sizes, rows),
         out_shape=(
             jax.ShapeDtypeStruct((2, 3, rows), F32),
-            jax.ShapeDtypeStruct((nz, 2 * span, rows, rows), BF16),
+            jax.ShapeDtypeStruct((nz, span, rows, rows), F8),
         ),
         in_specs=[vmem] * 4,
         out_specs=(vmem, pl.BlockSpec(memory_space=pltpu.HBM)),
@@ -495,9 +501,12 @@
             pltpu.VMEM((nx, 1, 128), F32),
             pltpu.VMEM((nz, 1, 128), F32),
             pltpu.VMEM((tiles, 3, rows, rows), BF16),
-            pltpu.VMEM((RING, 2 * span, rows, rows), BF16),
-            pltpu.VMEM((5, rows, rows), BF16),
-            pltpu.VMEM((5, rows, rows), BF16),
+            pltpu.VMEM((tiles, rows, rows), F8),
+            pltpu.VMEM((RING, span, rows, rows), F8),
+            pltpu.VMEM((3, rows, rows), BF16),
+            pltpu.VMEM((3, rows, rows), BF16),
+            pltpu.VMEM((2, rows, rows), F8),
+            pltpu.VMEM((2, rows, rows), F8),
             pltpu.VMEM((96, rows), BF16),
             pltpu.VMEM((96, rows), BF16),
             pltpu.VMEM((2, 96, rows), F32),

time: 115 us -> 110 us (0.957)
  Pallas kernels: 113 us -> 108 us
    pallas_call x1, Pallas kernels: 113 us -> 108 us  [on_device(): pl.pallas_call(functools.partial(kernel, sizes, rows), out_shape=(jax.Sha...]
where the time goes in v4:
time: 110 us
  Pallas kernels  108 us (98%)
  local copies, waits for them, and re-layouts  1.29 us (1%)
    pallas_call x1, Pallas kernels, on_device(): pl.pallas_call(functools.partial(kernel, sizes, rows), out_shape=(jax.Sha...  108 us

profile of v4, /device:TPU:40, one launch (start us, length us, event | category | flops | bytes accessed | tf_op | source)
XLA Modules:
  0.0 109.8 jit_solution(10876989490229573418)
XLA Ops:
  0.6 107.9 %shard_map.59 = (f32[2,3,256]{2,1,0:T(4,128)}, f8e4m3fn[16,8,256,256]{3,2,1,0:T(8,128)(4,1)}) custom-call(f32[3,256]{1,0:T(4,128)} %pos_ref.1, f32[3,256]{1,0:T(4,128)} %rhs_ref.1, s32[16,256]{1,0:T(8,128)} %nbr_ref.1, s32[1,256]{1,0:T(1,128)} %bitcast.5), custom_call_target="tpu_custom_call" | custom-call | tf_op jit(solution)/shard_map/pallas_call | solution.py:489
  108.5 1.3 %slice_bitcast_fusion = (f32[3,256]{1,0:T(4,128)}, f32[3,256]{1,0:T(4,128)}) fusion(f32[2,3,256]{2,1,0:T(4,128)} %get-tuple-element.3), kind=kLoop, calls=%fused_computation | loop fusion | bytes 12288 | tf_op jit(solution)/shard_map/squeeze | solution.py:526
